TPU v7x, 32 devices: a whole 2x2x4 slice. The times are simulated.
32 devices in a mesh: stage: 4 (over z), data: 8 (over y, x, core).
Axes of the slice: x: 2, y: 2, z: 4, core: 2. Of those that a mesh axis runs over, the one named last changes fastest.
Arguments:
- inputs: bfloat16 [32, 64, 768], P('data')
- targets: bfloat16 [32, 64, 768], P('data')
- w_up: bfloat16 [24, 768, 3072], P('stage')
- w_down: bfloat16 [24, 3072, 768], P('stage')
Outputs:
- output 1: float32 [], replicated
- output 2: float32 [24, 768, 3072], P('stage', 'data')
- output 3: float32 [24, 3072, 768], P('stage', None, 'data')
All inputs are finite; a program needn't handle non-finite values.
Results may differ from a plain program's by a relative error of at most 0.00946734.
Values are sent between devices in bfloat16 or wider.
A program may use at most 1 GiB of HBM per device.

v0:
```python
import jax
import jax.numpy as jnp
from jax import lax
from jax.sharding import PartitionSpec as P, NamedSharding

CONTRACT_ROWS = (((0,), (0,)), ((), ()))
CONTRACT_COLS = (((1,), (1,)), ((), ()))


def layer_forward(h_in, w_up, w_down):
    pre_act = jnp.dot(h_in, w_up, preferred_element_type=jnp.float32)
    gelu_out = jax.nn.gelu(pre_act).astype(jnp.bfloat16)
    branch = jnp.dot(gelu_out, w_down, preferred_element_type=jnp.float32)
    return (h_in.astype(jnp.float32) + branch).astype(jnp.bfloat16)


def layer_backward(h_in, grad_out, w_up, w_down):
    pre_act = jnp.dot(h_in, w_up, preferred_element_type=jnp.float32)
    gelu_full, gelu_vjp = jax.vjp(jax.nn.gelu, pre_act)
    gelu_out = gelu_full.astype(jnp.bfloat16)
    g_down = lax.dot_general(gelu_out, grad_out, CONTRACT_ROWS, preferred_element_type=jnp.float32)
    grad_act = lax.dot_general(grad_out, w_down, CONTRACT_COLS, preferred_element_type=jnp.float32).astype(jnp.bfloat16)
    grad_pre = gelu_vjp(grad_act.astype(jnp.float32))[0].astype(jnp.bfloat16)
    g_up = lax.dot_general(h_in, grad_pre, CONTRACT_ROWS, preferred_element_type=jnp.float32)
    back_prod = lax.dot_general(grad_pre, w_up, CONTRACT_COLS, preferred_element_type=jnp.float32)
    grad_in = (grad_out.astype(jnp.float32) + back_prod).astype(jnp.bfloat16)
    return grad_in, g_up, g_down


def solution(mesh):
    n_stage = mesh.shape['stage']
    n_data = mesh.shape['data']
    fwd_perm = [(k, k + 1) for k in range(n_stage - 1)]
    bwd_perm = [(k + 1, k) for k in range(n_stage - 1)]

    def per_device(inputs, targets, w_up, w_down):
        n_micro, n_tok, width = inputs.shape
        n_local = w_up.shape[0]
        stage_id = lax.axis_index('stage')
        is_first = stage_id == 0
        is_last = stage_id == n_stage - 1
        n_slots = min(n_micro, 2 * n_stage)
        inv_total = 1.0 / (n_data * n_micro * n_tok)

        def run_forward(h_first):
            layer_ins = []
            h_cur = h_first
            for layer_idx in range(n_local):
                layer_ins.append(h_cur)
                h_cur = layer_forward(h_cur, w_up[layer_idx], w_down[layer_idx])
            return h_cur, jnp.stack(layer_ins)

        def skip_forward(h_first):
            return jnp.zeros_like(h_first), jnp.zeros((n_local, n_tok, width), jnp.bfloat16)

        def run_backward(operands):
            grad_cur, saved_in, acc_up, acc_down = operands
            grads_up = []
            grads_down = []
            for layer_idx in reversed(range(n_local)):
                grad_cur, g_up, g_down = layer_backward(saved_in[layer_idx], grad_cur, w_up[layer_idx], w_down[layer_idx])
                grads_up.append(g_up)
                grads_down.append(g_down)
            return grad_cur, acc_up + jnp.stack(grads_up[::-1]), acc_down + jnp.stack(grads_down[::-1])

        def skip_backward(operands):
            return jnp.zeros_like(operands[0]), operands[2], operands[3]

        def tick(tick_idx, loop_state):
            recv_fwd, recv_bwd, last_grad, stash, acc_up, acc_down, loss_sum = loop_state
            fwd_mb = tick_idx - stage_id
            fwd_ok = (fwd_mb >= 0) & (fwd_mb < n_micro)
            fwd_row = jnp.clip(fwd_mb, 0, n_micro - 1)
            x_mb = lax.dynamic_index_in_dim(inputs, fwd_row, 0, keepdims=False)
            h_first = jnp.where(is_first, x_mb, recv_fwd)
            h_out, layer_ins = lax.cond(fwd_ok, run_forward, skip_forward, h_first)
            y_mb = lax.dynamic_index_in_dim(targets, fwd_row, 0, keepdims=False)
            resid_diff = h_out.astype(jnp.float32) - y_mb.astype(jnp.float32)
            loss_sum = loss_sum + jnp.where(fwd_ok & is_last, jnp.sum(resid_diff * resid_diff), 0.0)
            top_grad = (resid_diff * inv_total).astype(jnp.bfloat16)

            bwd_mb = tick_idx - (2 * n_stage - 1 - stage_id)
            bwd_ok = (bwd_mb >= 0) & (bwd_mb < n_micro)
            bwd_slot = jnp.where(bwd_ok, bwd_mb % n_slots, n_slots)
            saved_in = lax.dynamic_index_in_dim(stash, bwd_slot, 0, keepdims=False)
            grad_first = jnp.where(is_last, last_grad, recv_bwd)
            grad_out, acc_up, acc_down = lax.cond(bwd_ok, run_backward, skip_backward, (grad_first, saved_in, acc_up, acc_down))

            fwd_slot = jnp.where(fwd_ok, fwd_mb % n_slots, n_slots)
            stash = lax.dynamic_update_index_in_dim(stash, layer_ins, fwd_slot, 0)
            recv_fwd = lax.ppermute(h_out, 'stage', fwd_perm)
            recv_bwd = lax.ppermute(grad_out, 'stage', bwd_perm)
            return recv_fwd, recv_bwd, top_grad, stash, acc_up, acc_down, loss_sum

        zero_act = jnp.zeros((n_tok, width), jnp.bfloat16)
        init_state = (zero_act, zero_act, zero_act, jnp.zeros((n_slots + 1, n_local, n_tok, width), jnp.bfloat16), jnp.zeros(w_up.shape, jnp.float32), jnp.zeros(w_down.shape, jnp.float32), jnp.zeros((), jnp.float32))
        final_state = lax.fori_loop(0, n_micro + 2 * n_stage - 1, tick, init_state)
        grad_up = lax.psum_scatter(final_state[4], 'data', scatter_dimension=1, tiled=True)
        grad_down = lax.psum_scatter(final_state[5], 'data', scatter_dimension=2, tiled=True)
        loss_total = lax.psum(final_state[6], ('stage', 'data')) * (0.5 * inv_total)
        return loss_total, grad_up, grad_down

    return jax.shard_map(per_device, mesh=mesh, in_specs=(P('data', None, None), P('data', None, None), P('stage', None, None), P('stage', None, None)), out_specs=(P(), P('stage', 'data', None), P('stage', None, 'data')), check_vma=False)
```

profile of v0, /device:TPU:31, one launch (start us, length us, event | category | flops | bytes accessed | tf_op | source)
XLA Modules:
  0.0 2862.8 jit_solution(16467518674434771839)
XLA Ops:
  7.2 18.5 broadcast_in_dim.24
  25.7 17.9 broadcast_in_dim.25
  46.2 1888.1 %while.28 = (s32[]{:T(128)}, bf16[64,768]{1,0:T(8,128)(2,1)}, bf16[64,768]{1,0:T(8,128)(2,1)S(1)}, bf16[64,768]{1,0:T(8,128)(2,1)S(1)}, bf16[5,6,64,768]{3,2,1,0...) while((s32[]{:T(128)}, bf16[64,768]{1,0:T(8,128)(2,1)}, ...), condition=%wide.region_6.7_spmd.clone, body=%wide.region_0.6_spmd.clone.sunk | while | flops 12761432064 | bytes 639864000 | solution.py:97
  56.9 14.4 collective-permute-start.1
  77.7 35.7 %collective-permute-done = bf16[64,768]{1,0:T(8,128)(2,1)S(1)} collective-permute-done((bf16[64,768]{1,0:T(8,128)(2,1)S(1)}, bf16[64,768]{1,0:T(8,128)(2,1)S(1)}, u32[]{:S(2)}, u32[]{:S(2)}) %collective-permute-start) | collective-permute-done | bytes 98336 | tf_op jit(solution)/shard_map/while/body/eval_jaxpr/ppermute | solution.py:91
  114.7 41.6 %collective-permute-start.1 = (bf16[64,768]{1,0:T(8,128)(2,1)}, bf16[64,768]{1,0:T(8,128)(2,1)S(1)}, u32[]{:S(2)}, u32[]{:S(2)}) collective-permute-start(bf16[64,768]{1,0:T(8,128)(2,1)} %get-tuple-element.834), channel_id=1, source_target_pairs={{8,0},{16,8},{24,16},{9,1},{17,9},{25,17},{10,2},{18,10},{26,18},{... | collective-permute-start | bytes 294920 | tf_op jit(solution)/shard_map/while/body/eval_jaxpr/ppermute | solution.py:92
  162.6 38.6 %collective-permute-done = bf16[64,768]{1,0:T(8,128)(2,1)S(1)} collective-permute-done((bf16[64,768]{1,0:T(8,128)(2,1)S(1)}, bf16[64,768]{1,0:T(8,128)(2,1)S(1)}, u32[]{:S(2)}, u32[]{:S(2)}) %collective-permute-start) | collective-permute-done | bytes 98336 | tf_op jit(solution)/shard_map/while/body/eval_jaxpr/ppermute | solution.py:91
  206.6 38.9 %conditional.6 = (bf16[64,768]{1,0:T(8,128)(2,1)S(1)}, f32[64,768]{1,0:T(8,128)S(1)}, bf16[1,6,64,768]{3,2,1,0:T(8,128)(2,1)}) conditional(s32[]{:T(128)} %convert_element_type.508, () %tuple.95, (pred[]{:T(512)}, bf16[4,64,768]{2,1,0:T(8,128)(2,1)}, s32[]{:T(128)}, bf16[64,768]{1,0:T(8,128)(2,1)S(1)}, bf16[6,768,3072]{2,1,0:T(8,128)(2,1)}, ...), branch_computations={%region_1.1_spmd, %region_2.2_spmd} | conditional | flops 3635576832 | bytes 59574300 | solution.py:76
  208.2 6.3 bitcast_dynamic-update-slice_fusion.4
  214.6 6.3 bitcast_dynamic-update-slice_fusion.3
  220.9 6.3 bitcast_dynamic-update-slice_fusion.2
  227.2 6.3 bitcast_dynamic-update-slice_fusion.1
  233.5 6.3 bitcast_dynamic-update-slice_fusion
  251.6 246.5 %conditional.7 = (bf16[64,768]{1,0:T(8,128)(2,1)}, f32[6,768,3072]{2,1,0:T(8,128)}, f32[6,3072,768]{2,1,0:T(8,128)}) conditional(s32[]{:T(128)} %convert_element_type.509, (f32[6,768,3072]{2,1,0:T(8,128)}, f32[6,3072,768]{2,1,0:T(8,128)}) %tuple.97, (pred[]{:T(512)}, s32[]{:T(128)}, bf16[64,768]{1,0:T(8,128)(2,1)S(1)}, ...), branch_computations={%region_3.3_spmd, %region_4.4_spmd.clone} | conditional | flops 9125560320 | bytes 577143424 | solution.py:87
  344.2 55.1 %add.312 = f32[6,3072,768]{2,1,0:T(8,128)} add(f32[6,3072,768]{2,1,0:T(8,128)} %get-tuple-element.663, f32[6,3072,768]{2,1,0:T(8,128)} %bitcast_dynamic-update-slice_fusion.6) | non-fusion elementwise | flops 14155776 | bytes 169869312 | tf_op jit(solution)/shard_map/while/body/eval_jaxpr/cond/branch_1_fun/add | solution.py:64
  409.2 6.0 bitcast_dynamic-update-slice_fusion.16
  426.9 6.0 bitcast_dynamic-update-slice_fusion.13
  432.9 5.9 bitcast_dynamic-update-slice_fusion.12
  438.8 54.4 %add.311 = f32[6,768,3072]{2,1,0:T(8,128)} add(f32[6,768,3072]{2,1,0:T(8,128)} %get-tuple-element.662, f32[6,768,3072]{2,1,0:T(8,128)} %bitcast_dynamic-update-slice_fusion.12) | non-fusion elementwise | flops 14155776 | bytes 169869312 | tf_op jit(solution)/shard_map/while/body/eval_jaxpr/cond/branch_1_fun/add | solution.py:64
  499.5 38.9 %conditional.6 = (bf16[64,768]{1,0:T(8,128)(2,1)S(1)}, f32[64,768]{1,0:T(8,128)S(1)}, bf16[1,6,64,768]{3,2,1,0:T(8,128)(2,1)}) conditional(s32[]{:T(128)} %convert_element_type.508, () %tuple.95, (pred[]{:T(512)}, bf16[4,64,768]{2,1,0:T(8,128)(2,1)}, s32[]{:T(128)}, bf16[64,768]{1,0:T(8,128)(2,1)S(1)}, bf16[6,768,3072]{2,1,0:T(8,128)(2,1)}, ...), branch_computations={%region_1.1_spmd, %region_2.2_spmd} | conditional | flops 3635576832 | bytes 59574300 | solution.py:76
  501.0 6.3 bitcast_dynamic-update-slice_fusion.4
  507.4 6.3 bitcast_dynamic-update-slice_fusion.3
  513.7 6.3 bitcast_dynamic-update-slice_fusion.2
  520.0 6.3 bitcast_dynamic-update-slice_fusion.1
  526.3 6.3 bitcast_dynamic-update-slice_fusion
  544.6 246.3 %conditional.7 = (bf16[64,768]{1,0:T(8,128)(2,1)}, f32[6,768,3072]{2,1,0:T(8,128)}, f32[6,3072,768]{2,1,0:T(8,128)}) conditional(s32[]{:T(128)} %convert_element_type.509, (f32[6,768,3072]{2,1,0:T(8,128)}, f32[6,3072,768]{2,1,0:T(8,128)}) %tuple.97, (pred[]{:T(512)}, s32[]{:T(128)}, bf16[64,768]{1,0:T(8,128)(2,1)S(1)}, ...), branch_computations={%region_3.3_spmd, %region_4.4_spmd.clone} | conditional | flops 9125560320 | bytes 577143424 | solution.py:87
  637.0 55.3 %add.312 = f32[6,3072,768]{2,1,0:T(8,128)} add(f32[6,3072,768]{2,1,0:T(8,128)} %get-tuple-element.663, f32[6,3072,768]{2,1,0:T(8,128)} %bitcast_dynamic-update-slice_fusion.6) | non-fusion elementwise | flops 14155776 | bytes 169869312 | tf_op jit(solution)/shard_map/while/body/eval_jaxpr/cond/branch_1_fun/add | solution.py:64
  702.2 6.0 bitcast_dynamic-update-slice_fusion.16
  720.0 6.0 bitcast_dynamic-update-slice_fusion.13
  725.9 5.9 bitcast_dynamic-update-slice_fusion.12
  731.8 54.4 %add.311 = f32[6,768,3072]{2,1,0:T(8,128)} add(f32[6,768,3072]{2,1,0:T(8,128)} %get-tuple-element.662, f32[6,768,3072]{2,1,0:T(8,128)} %bitcast_dynamic-update-slice_fusion.12) | non-fusion elementwise | flops 14155776 | bytes 169869312 | tf_op jit(solution)/shard_map/while/body/eval_jaxpr/cond/branch_1_fun/add | solution.py:64
  795.0 38.9 %conditional.6 = (bf16[64,768]{1,0:T(8,128)(2,1)S(1)}, f32[64,768]{1,0:T(8,128)S(1)}, bf16[1,6,64,768]{3,2,1,0:T(8,128)(2,1)}) conditional(s32[]{:T(128)} %convert_element_type.508, () %tuple.95, (pred[]{:T(512)}, bf16[4,64,768]{2,1,0:T(8,128)(2,1)}, s32[]{:T(128)}, bf16[64,768]{1,0:T(8,128)(2,1)S(1)}, bf16[6,768,3072]{2,1,0:T(8,128)(2,1)}, ...), branch_computations={%region_1.1_spmd, %region_2.2_spmd} | conditional | flops 3635576832 | bytes 59574300 | solution.py:76
  796.5 6.3 bitcast_dynamic-update-slice_fusion.4
  802.9 6.3 bitcast_dynamic-update-slice_fusion.3
  809.2 6.3 bitcast_dynamic-update-slice_fusion.2
  815.5 6.3 bitcast_dynamic-update-slice_fusion.1
  821.9 6.3 bitcast_dynamic-update-slice_fusion
  840.2 246.3 %conditional.7 = (bf16[64,768]{1,0:T(8,128)(2,1)}, f32[6,768,3072]{2,1,0:T(8,128)}, f32[6,3072,768]{2,1,0:T(8,128)}) conditional(s32[]{:T(128)} %convert_element_type.509, (f32[6,768,3072]{2,1,0:T(8,128)}, f32[6,3072,768]{2,1,0:T(8,128)}) %tuple.97, (pred[]{:T(512)}, s32[]{:T(128)}, bf16[64,768]{1,0:T(8,128)(2,1)S(1)}, ...), branch_computations={%region_3.3_spmd, %region_4.4_spmd.clone} | conditional | flops 9125560320 | bytes 577143424 | solution.py:87
  932.8 55.0 %add.312 = f32[6,3072,768]{2,1,0:T(8,128)} add(f32[6,3072,768]{2,1,0:T(8,128)} %get-tuple-element.663, f32[6,3072,768]{2,1,0:T(8,128)} %bitcast_dynamic-update-slice_fusion.6) | non-fusion elementwise | flops 14155776 | bytes 169869312 | tf_op jit(solution)/shard_map/while/body/eval_jaxpr/cond/branch_1_fun/add | solution.py:64
  997.8 6.0 bitcast_dynamic-update-slice_fusion.16
  1015.5 6.0 bitcast_dynamic-update-slice_fusion.13
  1021.4 5.9 bitcast_dynamic-update-slice_fusion.12
  1027.3 54.4 %add.311 = f32[6,768,3072]{2,1,0:T(8,128)} add(f32[6,768,3072]{2,1,0:T(8,128)} %get-tuple-element.662, f32[6,768,3072]{2,1,0:T(8,128)} %bitcast_dynamic-update-slice_fusion.12) | non-fusion elementwise | flops 14155776 | bytes 169869312 | tf_op jit(solution)/shard_map/while/body/eval_jaxpr/cond/branch_1_fun/add | solution.py:64
  1090.5 38.9 %conditional.6 = (bf16[64,768]{1,0:T(8,128)(2,1)S(1)}, f32[64,768]{1,0:T(8,128)S(1)}, bf16[1,6,64,768]{3,2,1,0:T(8,128)(2,1)}) conditional(s32[]{:T(128)} %convert_element_type.508, () %tuple.95, (pred[]{:T(512)}, bf16[4,64,768]{2,1,0:T(8,128)(2,1)}, s32[]{:T(128)}, bf16[64,768]{1,0:T(8,128)(2,1)S(1)}, bf16[6,768,3072]{2,1,0:T(8,128)(2,1)}, ...), branch_computations={%region_1.1_spmd, %region_2.2_spmd} | conditional | flops 3635576832 | bytes 59574300 | solution.py:76
  1092.1 6.3 bitcast_dynamic-update-slice_fusion.4
  1098.4 6.3 bitcast_dynamic-update-slice_fusion.3
  1104.7 6.3 bitcast_dynamic-update-slice_fusion.2
  1111.1 6.3 bitcast_dynamic-update-slice_fusion.1
  1117.4 6.3 bitcast_dynamic-update-slice_fusion
  1135.9 246.3 %conditional.7 = (bf16[64,768]{1,0:T(8,128)(2,1)}, f32[6,768,3072]{2,1,0:T(8,128)}, f32[6,3072,768]{2,1,0:T(8,128)}) conditional(s32[]{:T(128)} %convert_element_type.509, (f32[6,768,3072]{2,1,0:T(8,128)}, f32[6,3072,768]{2,1,0:T(8,128)}) %tuple.97, (pred[]{:T(512)}, s32[]{:T(128)}, bf16[64,768]{1,0:T(8,128)(2,1)S(1)}, ...), branch_computations={%region_3.3_spmd, %region_4.4_spmd.clone} | conditional | flops 9125560320 | bytes 577143424 | solution.py:87
  1228.3 55.1 %add.312 = f32[6,3072,768]{2,1,0:T(8,128)} add(f32[6,3072,768]{2,1,0:T(8,128)} %get-tuple-element.663, f32[6,3072,768]{2,1,0:T(8,128)} %bitcast_dynamic-update-slice_fusion.6) | non-fusion elementwise | flops 14155776 | bytes 169869312 | tf_op jit(solution)/shard_map/while/body/eval_jaxpr/cond/branch_1_fun/add | solution.py:64
  1293.3 6.0 bitcast_dynamic-update-slice_fusion.16
  1311.0 6.0 bitcast_dynamic-update-slice_fusion.13
  1317.0 5.9 bitcast_dynamic-update-slice_fusion.12
  1322.9 54.4 %add.311 = f32[6,768,3072]{2,1,0:T(8,128)} add(f32[6,768,3072]{2,1,0:T(8,128)} %get-tuple-element.662, f32[6,768,3072]{2,1,0:T(8,128)} %bitcast_dynamic-update-slice_fusion.12) | non-fusion elementwise | flops 14155776 | bytes 169869312 | tf_op jit(solution)/shard_map/while/body/eval_jaxpr/cond/branch_1_fun/add | solution.py:64
  1393.2 14.3 conditional.7
  1407.5 236.3 %collective-permute-start.1 = (bf16[64,768]{1,0:T(8,128)(2,1)}, bf16[64,768]{1,0:T(8,128)(2,1)S(1)}, u32[]{:S(2)}, u32[]{:S(2)}) collective-permute-start(bf16[64,768]{1,0:T(8,128)(2,1)} %get-tuple-element.834), channel_id=1, source_target_pairs={{8,0},{16,8},{24,16},{9,1},{17,9},{25,17},{10,2},{18,10},{26,18},{... | collective-permute-start | bytes 294920 | tf_op jit(solution)/shard_map/while/body/eval_jaxpr/ppermute | solution.py:92
  1651.5 17.8 collective-permute-start.1
  1675.7 230.7 %collective-permute-done = bf16[64,768]{1,0:T(8,128)(2,1)S(1)} collective-permute-done((bf16[64,768]{1,0:T(8,128)(2,1)S(1)}, bf16[64,768]{1,0:T(8,128)(2,1)S(1)}, u32[]{:S(2)}, u32[]{:S(2)}) %collective-permute-start) | collective-permute-done | bytes 98336 | tf_op jit(solution)/shard_map/while/body/eval_jaxpr/ppermute | solution.py:91
  1918.2 13.7 collective-permute-done
  1934.3 54.9 %copy.7 = f32[6,3072,768]{1,2,0:T(8,128)} copy(f32[6,3072,768]{2,1,0:T(8,128)} %get-tuple-element.588) | data formatting | bytes 113246208 | tf_op jit(solution)/shard_map/while | solution.py:97
  1990.0 278.1 %psum.7 = f32[]{:T(128)} all-reduce(f32[]{:T(128)} %get-tuple-element.586), channel_id=1, replica_groups=mesh['stage'=4,'data'=8] {'stage','data'}, use_global_device_ids=true, to_apply=%region_7.8 | all-reduce | flops 1 | bytes 8 | tf_op jit(solution)/shard_map/psum | solution.py:100
  2268.7 270.0 %reduce-scatter.5.cloned.1.call-done = f32[6,3072,96]{1,2,0:T(8,128)} async-done(((f32[6,3072,768]{1,2,0:T(8,128)}), f32[6,3072,96]{1,2,0:T(8,128)}) %reduce-scatter.5.cloned.1.call-update) | async-done | bytes 7077904 | tf_op jit(solution)/shard_map/reduce_scatter | solution.py:99
  2538.7 315.7 %reduce-scatter.3.cloned.1.call-done = f32[6,96,3072]{2,1,0:T(8,128)} async-done(((f32[6,768,3072]{2,1,0:T(8,128)}), f32[6,96,3072]{2,1,0:T(8,128)}) %reduce-scatter.3.cloned.1.call-update) | async-done | bytes 7077904 | tf_op jit(solution)/shard_map/reduce_scatter | solution.py:98
  (367 shorter events, 610.2 us)
Async XLA Ops:
  7.2 2531.6 %reduce-scatter.5.cloned.1.call-start = ((), (), s32[]{:S(2)}) async-start(), calls=%async_computation.3 | async-start | bytes 63700992 | tf_op jit(solution)/shard_map/reduce_scatter | solution.py:99
  47.1 8.5 collective-permute-start.1
  50.1 5.5 collective-permute-start
  56.2 15.1 copy-start.8
  56.9 20.8 collective-permute-start.1
  72.2 41.1 %collective-permute-start = (bf16[64,768]{1,0:T(8,128)(2,1)S(1)}, bf16[64,768]{1,0:T(8,128)(2,1)S(1)}, u32[]{:S(2)}, u32[]{:S(2)}) collective-permute-start(bf16[64,768]{1,0:T(8,128)(2,1)S(1)} %get-tuple-element.833), channel_id=1, source_target_pairs={{0,8},{8,16},{16,24},{1,9},{9,17},{17,25},{2,10},{10,18},{18,26},{... | collective-permute-start | bytes 294920 | tf_op jit(solution)/shard_map/while/body/eval_jaxpr/ppermute | solution.py:91
  114.0 42.2 %copy-start.8 = (bf16[64,768]{1,0:T(8,128)(2,1)S(1)}, bf16[64,768]{1,0:T(8,128)(2,1)}, u32[]{:S(2)}) copy-start(bf16[64,768]{1,0:T(8,128)(2,1)} %get-tuple-element.876) | copy-start | bytes 294916 | tf_op jit(solution)/shard_map/while
  114.7 48.0 %collective-permute-start.1 = (bf16[64,768]{1,0:T(8,128)(2,1)}, bf16[64,768]{1,0:T(8,128)(2,1)S(1)}, u32[]{:S(2)}, u32[]{:S(2)}) collective-permute-start(bf16[64,768]{1,0:T(8,128)(2,1)} %get-tuple-element.834), channel_id=1, source_target_pairs={{8,0},{16,8},{24,16},{9,1},{17,9},{25,17},{10,2},{18,10},{26,18},{... | collective-permute-start | bytes 294920 | tf_op jit(solution)/shard_map/while/body/eval_jaxpr/ppermute | solution.py:92
  157.2 44.1 %collective-permute-start = (bf16[64,768]{1,0:T(8,128)(2,1)S(1)}, bf16[64,768]{1,0:T(8,128)(2,1)S(1)}, u32[]{:S(2)}, u32[]{:S(2)}) collective-permute-start(bf16[64,768]{1,0:T(8,128)(2,1)S(1)} %get-tuple-element.833), channel_id=1, source_target_pairs={{0,8},{8,16},{16,24},{1,9},{9,17},{17,25},{2,10},{10,18},{18,26},{... | collective-permute-start | bytes 294920 | tf_op jit(solution)/shard_map/while/body/eval_jaxpr/ppermute | solution.py:91
  202.5 48.5 %collective-permute-start.1 = (bf16[64,768]{1,0:T(8,128)(2,1)}, bf16[64,768]{1,0:T(8,128)(2,1)S(1)}, u32[]{:S(2)}, u32[]{:S(2)}) collective-permute-start(bf16[64,768]{1,0:T(8,128)(2,1)} %get-tuple-element.834), channel_id=1, source_target_pairs={{8,0},{16,8},{24,16},{9,1},{17,9},{25,17},{10,2},{18,10},{26,18},{... | collective-permute-start | bytes 294920 | tf_op jit(solution)/shard_map/while/body/eval_jaxpr/ppermute | solution.py:92
  245.5 5.5 collective-permute-start
  251.6 247.8 %copy-start.8 = (bf16[64,768]{1,0:T(8,128)(2,1)S(1)}, bf16[64,768]{1,0:T(8,128)(2,1)}, u32[]{:S(2)}) copy-start(bf16[64,768]{1,0:T(8,128)(2,1)} %get-tuple-element.876) | copy-start | bytes 294916 | tf_op jit(solution)/shard_map/while
  274.3 28.0 copy-start.10
  299.0 20.0 copy-start.13
  299.0 25.1 copy-start.12
  306.7 22.4 copy-start.11
  399.2 15.9 copy-start.7
  399.2 21.8 copy-start.5
  403.3 23.6 copy-start.3
  409.2 23.7 copy-start.1
  498.1 45.7 %collective-permute-start.1 = (bf16[64,768]{1,0:T(8,128)(2,1)}, bf16[64,768]{1,0:T(8,128)(2,1)S(1)}, u32[]{:S(2)}, u32[]{:S(2)}) collective-permute-start(bf16[64,768]{1,0:T(8,128)(2,1)} %get-tuple-element.834), channel_id=1, source_target_pairs={{8,0},{16,8},{24,16},{9,1},{17,9},{25,17},{10,2},{18,10},{26,18},{... | collective-permute-start | bytes 294920 | tf_op jit(solution)/shard_map/while/body/eval_jaxpr/ppermute | solution.py:92
  538.3 5.5 collective-permute-start
  544.6 250.3 %copy-start.8 = (bf16[64,768]{1,0:T(8,128)(2,1)S(1)}, bf16[64,768]{1,0:T(8,128)(2,1)}, u32[]{:S(2)}) copy-start(bf16[64,768]{1,0:T(8,128)(2,1)} %get-tuple-element.876) | copy-start | bytes 294916 | tf_op jit(solution)/shard_map/while
  567.3 28.0 copy-start.10
  592.0 19.8 copy-start.13
  592.0 24.9 copy-start.12
  599.6 22.4 copy-start.11
  692.3 16.0 copy-start.7
  692.3 21.8 copy-start.5
  696.3 23.6 copy-start.3
  702.2 23.7 copy-start.1
  790.9 48.4 %collective-permute-start.1 = (bf16[64,768]{1,0:T(8,128)(2,1)}, bf16[64,768]{1,0:T(8,128)(2,1)S(1)}, u32[]{:S(2)}, u32[]{:S(2)}) collective-permute-start(bf16[64,768]{1,0:T(8,128)(2,1)} %get-tuple-element.834), channel_id=1, source_target_pairs={{8,0},{16,8},{24,16},{9,1},{17,9},{25,17},{10,2},{18,10},{26,18},{... | collective-permute-start | bytes 294920 | tf_op jit(solution)/shard_map/while/body/eval_jaxpr/ppermute | solution.py:92
  833.9 5.5 collective-permute-start
  840.2 250.3 %copy-start.8 = (bf16[64,768]{1,0:T(8,128)(2,1)S(1)}, bf16[64,768]{1,0:T(8,128)(2,1)}, u32[]{:S(2)}) copy-start(bf16[64,768]{1,0:T(8,128)(2,1)} %get-tuple-element.876) | copy-start | bytes 294916 | tf_op jit(solution)/shard_map/while
  862.9 28.0 copy-start.10
  887.5 20.0 copy-start.13
  887.5 25.1 copy-start.12
  895.3 22.4 copy-start.11
  987.8 15.9 copy-start.7
  987.8 21.8 copy-start.5
  991.8 23.6 copy-start.3
  997.7 23.7 copy-start.1
  1086.5 48.3 %collective-permute-start.1 = (bf16[64,768]{1,0:T(8,128)(2,1)}, bf16[64,768]{1,0:T(8,128)(2,1)S(1)}, u32[]{:S(2)}, u32[]{:S(2)}) collective-permute-start(bf16[64,768]{1,0:T(8,128)(2,1)} %get-tuple-element.834), channel_id=1, source_target_pairs={{8,0},{16,8},{24,16},{9,1},{17,9},{25,17},{10,2},{18,10},{26,18},{... | collective-permute-start | bytes 294920 | tf_op jit(solution)/shard_map/while/body/eval_jaxpr/ppermute | solution.py:92
  1129.4 5.5 collective-permute-start
  1135.9 250.2 %copy-start.8 = (bf16[64,768]{1,0:T(8,128)(2,1)S(1)}, bf16[64,768]{1,0:T(8,128)(2,1)}, u32[]{:S(2)}) copy-start(bf16[64,768]{1,0:T(8,128)(2,1)} %get-tuple-element.876) | copy-start | bytes 294916 | tf_op jit(solution)/shard_map/while
  1158.6 28.0 copy-start.10
  1183.2 19.8 copy-start.13
  1183.2 24.9 copy-start.12
  1190.8 22.4 copy-start.11
  1283.3 15.9 copy-start.7
  1283.3 21.8 copy-start.5
  1287.4 23.6 copy-start.3
  1293.3 23.7 copy-start.1
  1382.2 10.2 collective-permute-start.1
  1387.0 5.5 collective-permute-start
  1393.2 250.6 %copy-start.8 = (bf16[64,768]{1,0:T(8,128)(2,1)S(1)}, bf16[64,768]{1,0:T(8,128)(2,1)}, u32[]{:S(2)}) copy-start(bf16[64,768]{1,0:T(8,128)(2,1)} %get-tuple-element.876) | copy-start | bytes 294916 | tf_op jit(solution)/shard_map/while
  1407.5 242.7 %collective-permute-start.1 = (bf16[64,768]{1,0:T(8,128)(2,1)}, bf16[64,768]{1,0:T(8,128)(2,1)S(1)}, u32[]{:S(2)}, u32[]{:S(2)}) collective-permute-start(bf16[64,768]{1,0:T(8,128)(2,1)} %get-tuple-element.834), channel_id=1, source_target_pairs={{8,0},{16,8},{24,16},{9,1},{17,9},{25,17},{10,2},{18,10},{26,18},{... | collective-permute-start | bytes 294920 | tf_op jit(solution)/shard_map/while/body/eval_jaxpr/ppermute | solution.py:92
  1644.7 5.5 collective-permute-start
  1650.8 18.5 copy-start.8
  1651.5 24.2 collective-permute-start.1
  1670.2 236.2 %collective-permute-start = (bf16[64,768]{1,0:T(8,128)(2,1)S(1)}, bf16[64,768]{1,0:T(8,128)(2,1)S(1)}, u32[]{:S(2)}, u32[]{:S(2)}) collective-permute-start(bf16[64,768]{1,0:T(8,128)(2,1)S(1)} %get-tuple-element.833), channel_id=1, source_target_pairs={{0,8},{8,16},{16,24},{1,9},{9,17},{17,25},{2,10},{10,18},{18,26},{... | collective-permute-start | bytes 294920 | tf_op jit(solution)/shard_map/while/body/eval_jaxpr/ppermute | solution.py:91
  1907.7 10.5 collective-permute-start.1
  1912.7 19.2 collective-permute-start
  1989.2 865.3 %reduce-scatter.3.cloned.1.call-start = ((), (), s32[]{:S(2)}) async-start(), calls=%async_computation.2 | async-start | bytes 63700992 | tf_op jit(solution)/shard_map/reduce_scatter | solution.py:98
  (30 other events, 73.4 us)
Sparse Core Ops, SparseCore 0:
  1989.3 549.3 reduce-scatter.4
  2543.0 311.4 reduce-scatter.2
where the time goes:
time: 2870 us; the launch traced here: 2860 us
  waiting for transfers between devices  905 us (32%)
  matrix products  691 us (24%)
  other arithmetic  462 us (16%)
  starting transfers between devices  348 us (12%)
  blocking collectives  278 us (10%)
  local copies, waits for them, and re-layouts  136 us (5%)
    ppermute x11, starting transfers between devices, tick(): recv_bwd = lax.ppermute(grad_out, 'stage', bwd_perm)  333 us
    ppermute x11, waiting for transfers between devices, tick(): recv_fwd = lax.ppermute(h_out, 'stage', fwd_perm)  319 us
    reduce_scatter x1, waiting for transfers between devices, per_device(): lax.psum_scatter(final_state[4], 'data', scatter_dimension=1, tiled=True)  316 us
    psum x1, blocking collectives, per_device(): loss_total = lax.psum(final_state[6], ('stage', 'data')) * (0.5 * inv_total)  278 us
    reduce_scatter x1, waiting for transfers between devices, per_device(): lax.psum_scatter(final_state[5], 'data', scatter_dimension=2, tiled=True)  270 us
    add x4, other arithmetic, run_backward(): acc_down + jnp.stack(grads_down[::-1])  220 us
    add x4, other arithmetic, run_backward(): acc_up + jnp.stack(grads_up[::-1])  218 us
    dot_general x24, matrix products, layer_forward(): branch = jnp.dot(gelu_out, w_down, preferred_element_type=jnp.float32)  149 us
  transfers between devices with their start and end apart: 24, of which 6 were waited for; matrix products, arithmetic and copies ran while one was open for 7% of the time, Pallas kernels for 0%

commit v1 on v0

v1 whole, which is shorter than its diff:
```python
import functools

import jax
import jax.numpy as jnp
from jax import lax
from jax.experimental import pallas as pl
from jax.experimental.pallas import tpu as pltpu
from jax.sharding import PartitionSpec as P

bf16, f32 = jnp.bfloat16, jnp.float32
MESH = pl.DeviceIdType.MESH
NT = (((1,), (1,)), ((), ()))
C0 = 0.7978845608028654
C1 = C0 * 0.044715
D, F = 768, 3072
CH, PR = 128, 256
NL = 3
DS = 192
FB = 768
NSTEP = 18


def dot(a, b):
    return jnp.dot(a, b, preferred_element_type=f32)


def dot_nt(a, b):
    return lax.dot_general(a, b, NT, preferred_element_type=f32)


def gelu(u):
    t = jnp.tanh(u * (C0 + C1 * (u * u)))
    hu = 0.5 * u
    return hu + hu * t


def gelu_and_slope(u):
    s = u * u
    t = jnp.tanh(u * (C0 + C1 * s))
    a = 1.0 + t
    g = (0.5 * u) * a
    return g, 0.5 * a + g * ((1.0 - t) * (C0 + (3.0 * C1) * s))


def kernel(inv_total, x_in, y_in, w_up, w_down,
           loss_out, out_up, out_down, u_hbm,
           w1, w2, hs, es, acc1, acc2, ub, gs, qs, hT, hcur, ecur, eout, tgt, sel, ltile, lbuf, lmine,
           wsem, hrecv, erecv, trecv, lrecv, xsend, hfwd, efwd, hsend, esend, tsend, lsend, lchain_s, lchain_r,
           osem, isem, xo_s, xo_r, lo_s):
    s = lax.axis_index("stage")
    d = lax.axis_index("data")
    c = d % 2
    q = d // 2
    k = 2 * s + c
    nxt = (s + c, d + 1 - 2 * c)
    prv = (s - 1 + c, d + 1 - 2 * c)
    partner = (s, d + 1 - 2 * c)
    peers = [(s, ((q + p) % 4) * 2 + c) for p in (1, 2, 3)]

    def rcopy(src, dst, ss, rs, dev):
        return pltpu.make_async_remote_copy(src_ref=src, dst_ref=dst, send_sem=ss, recv_sem=rs, device_id=dev, device_id_type=MESH)

    def lcopy(src, dst, sem):
        return pltpu.make_async_copy(src, dst, sem)

    bar = pltpu.get_barrier_semaphore()
    for dev in peers:
        pl.semaphore_signal(bar, inc=1, device_id=dev, device_id_type=MESH)

    @pl.when(k < 7)
    def _():
        pl.semaphore_signal(bar, inc=1, device_id=nxt, device_id_type=MESH)

    @pl.when(k > 0)
    def _():
        pl.semaphore_signal(bar, inc=1, device_id=prv, device_id_type=MESH)

    def wcopy(l, m):
        if m == 0:
            return lcopy(w_up.at[NL * c + l], w1.at[l], wsem.at[l, 0])
        return lcopy(w_down.at[NL * c + l], w2.at[l], wsem.at[l, 1])

    for l in range(NL):
        for m in range(2):
            wcopy(l, m).start()

    def slot(ref, ch):
        return ref.at[ch // 2, pl.ds(pl.multiple_of((ch % 2) * CH, CH), CH), :]

    own0 = 4 * q

    @pl.when(k == 0)
    def _():
        for j in range(2):
            lcopy(x_in.at[pl.ds(j * CH, CH), :], slot(hs, own0 + j), hrecv.at[own0 + j]).start()

    @pl.when(k == 7)
    def _():
        lcopy(y_in, tgt.at[1], trecv.at[1]).start()

    row = lax.broadcasted_iota(jnp.int32, (DS, D), 0)
    col = lax.broadcasted_iota(jnp.int32, (DS, D), 1)
    sel[...] = jnp.where(col == row + DS * q, 1.0, 0.0).astype(bf16)
    ltile[...] = jnp.zeros_like(ltile)

    def zero(i, carry):
        r = pl.ds(pl.multiple_of(i * 8, 8), 8)
        for l in range(NL):
            acc1[l, r, :] = jnp.zeros((8, F), f32)
            acc2[l, r, :] = jnp.zeros((8, F), f32)
        return carry

    lax.fori_loop(0, DS // 8, zero, 0)

    pl.semaphore_wait(bar, 3 + jnp.where(k < 7, 1, 0) + jnp.where(k > 0, 1, 0))

    def xcopy(j):
        return rcopy(x_in.at[pl.ds(j * CH, CH), :], slot(hs, own0 + 2 + j), xsend.at[j], hrecv.at[own0 + 2 + j], partner)

    def tcopy():
        return rcopy(y_in, tgt.at[0], tsend.at[0], trecv.at[0], partner)

    @pl.when(k == 1)
    def _():
        xcopy(0).start()
        xcopy(1).start()

    @pl.when(k == 6)
    def _():
        tcopy().start()

    def h_fwd(j, p):
        ch = own0 + j
        return rcopy(slot(hs, ch), slot(hs, ch), hfwd.at[j, p], hrecv.at[ch], peers[p])

    def e_fwd(jp, p):
        pr = 2 * q + jp
        return rcopy(es.at[pr], es.at[pr], efwd.at[jp, p], erecv.at[pr], peers[p])

    def h_out(j):
        return rcopy(slot(tgt, j), slot(hs, own0 + j), hsend.at[j], hrecv.at[own0 + j], nxt)

    def e_out(jp):
        return rcopy(eout.at[jp], es.at[2 * q + jp], esend.at[jp], erecv.at[2 * q + jp], prv)

    def l_peer(p):
        return rcopy(lmine, lbuf.at[q], lsend.at[p], lrecv.at[q], peers[p])

    def l_chain():
        return rcopy(loss_out, loss_out, lchain_s, lchain_r, prv)

    def wait_h(ch):
        rcopy(slot(hs, ch), slot(hs, ch), hfwd.at[0, 0], hrecv.at[ch], peers[0]).wait_recv()

    def wait_e(pr):
        rcopy(es.at[pr], es.at[pr], efwd.at[0, 0], erecv.at[pr], peers[0]).wait_recv()

    def u_out_own(l, ch, b):
        return lcopy(ub.at[b, pl.ds(0, CH), :], u_hbm.at[l, ch // 2, pl.ds(pl.multiple_of((ch % 2) * CH, CH), CH), :], osem.at[b])

    def u_out(l, pr, b):
        return lcopy(ub.at[b], u_hbm.at[l, pr], osem.at[b])

    def u_in(l, pr, b):
        return lcopy(u_hbm.at[l, pr], ub.at[b], isem.at[b])

    early = jnp.where(k == 6, 1, jnp.minimum(6, 2 * (7 - k)))
    last = k == 7

    def is_f_own(t):
        return jnp.where(last, (t < 2) | (t == 3) | (t == 4), t < 4)

    def f_own_j(t):
        return jnp.where(last & (t > 2), t - 1, t)

    def is_b_own(t):
        return jnp.where(last, (t == 2) | (t == 5), (t >= 4 + early) & (t < 6 + early))

    def b_own_j(t):
        return jnp.where(last, t // 4, t - 4 - early)

    def is_b_oth(t):
        return (t >= 12) & (t < NSTEP)

    def is_b(t):
        return is_b_own(t) | is_b_oth(t)

    def is_f_oth(t):
        return jnp.logical_not(is_f_own(t) | is_b(t)) & (t >= 2)

    def f_oth_i(t):
        return jnp.where(last, t - 6, jnp.where(t < 4 + early, t - 4, t - 6))

    def oth_pair(i):
        return 2 * ((q + 1 + i % 3) % 4) + i // 3

    def b_pair(t):
        return jnp.where(is_b_own(t), 2 * q + b_own_j(t), oth_pair(t - 12))

    def up_half(l, M, pr, off, b):
        h = hcur[0:M, :]
        hT[l, pr, :, pl.ds(off, M)] = dot_nt(sel[...], h).astype(bf16)
        for i in range(F // FB):
            o = i * FB
            u = dot(h, w1[l, :, o:o + FB])
            ub[b, 0:M, o:o + FB] = u
            gs[0:M, o:o + FB] = gelu(u).astype(bf16)

    def down_half(l, M):
        v = dot(gs[0:M, :], w2[l])
        hcur[0:M, :] = (hcur[0:M, :].astype(f32) + v).astype(bf16)

    def f_own(t):
        j = f_own_j(t)
        ch = own0 + j
        wait_h(ch)
        for p in range(3):
            h_fwd(j, p).start()
        off = pl.multiple_of((j % 2) * CH, CH)
        hcur[0:CH, :] = hs[ch // 2, pl.ds(off, CH), :]

        def layer(l, carry):
            b = l % 2

            @pl.when(t == 0)
            def _():
                lcopy(w_up.at[NL * c + l], w1.at[l], wsem.at[l, 0]).wait()
                lcopy(w_down.at[NL * c + l], w2.at[l], wsem.at[l, 1]).wait()

            @pl.when(l == 2)
            def _():
                u_out_own(0, ch, 0).wait()

            up_half(l, CH, ch // 2, off, b)
            u_out_own(l, ch, b).start()
            down_half(l, CH)
            return carry

        lax.fori_loop(0, NL, layer, 0)

        @pl.when(k < 7)
        def _():
            tgt[j // 2, pl.ds(off, CH), :] = hcur[0:CH, :]
            h_out(j).start()

        @pl.when(k == 7)
        def _():
            @pl.when(j == 0)
            def _():
                rcopy(y_in, tgt.at[0], tsend.at[0], trecv.at[0], partner).wait_recv()

            @pl.when(j == 2)
            def _():
                lcopy(y_in, tgt.at[1], trecv.at[1]).wait()

            diff = hcur[0:CH, :].astype(f32) - tgt[j // 2, pl.ds(off, CH), :].astype(f32)
            es[ch // 2, pl.ds(off, CH), :] = (diff * inv_total).astype(bf16)
            sq = jnp.sum((diff * diff).reshape(CH // 8, 8, D), axis=0)
            ltile[...] += sum(sq[:, i * 128:(i + 1) * 128] for i in range(D // 128))

            @pl.when(j == 3)
            def _():
                lmine[...] = ltile[...]

        u_out_own(1, ch, 1).wait()
        u_out_own(2, ch, 0).wait()

    def f_oth(t):
        pr = oth_pair(f_oth_i(t))
        wait_h(2 * pr)
        wait_h(2 * pr + 1)
        hcur[...] = hs[pr]

        def layer(l, carry):
            b = (t + l) % 2

            @pl.when((l == 1) & is_f_oth(t - 1))
            def _():
                u_out(2, 0, b).wait()

            @pl.when(l == 2)
            def _():
                u_out(0, pr, b).wait()

            up_half(l, PR, pr, 0, b)
            u_out(l, pr, b).start()

            @pl.when(l < 2)
            def _():
                down_half(l, PR)

            return carry

        lax.fori_loop(0, NL, layer, 0)
        u_out(1, pr, (t + 1) % 2).wait()

    def b_step(t):
        own = is_b_own(t)
        jp = b_own_j(t)
        pr = b_pair(t)

        @pl.when(is_f_oth(t - 1))
        def _():
            u_out(2, 0, (t + 1) % 2).wait()

        @pl.when(jnp.logical_not(is_b(t - 1)))
        def _():
            u_in(2, pr, t % 2).start()

        @pl.when(jnp.logical_not(own & last))
        def _():
            wait_e(pr)

        ecur[...] = es[pr]

        def layer(li, carry):
            l = 2 - li
            b = (t + li) % 2
            u_in(l, pr, b).wait()

            @pl.when(li < 2)
            def _():
                u_in(l - 1, pr, 1 - b).start()

            @pl.when((li == 2) & is_b(t + 1))
            def _():
                u_in(2, b_pair(t + 1), 1 - b).start()

            e = ecur[...]
            eT = dot_nt(sel[...], e).astype(bf16)
            hTl = hT[l, pr]
            for i in range(F // FB):
                o = i * FB
                p = dot_nt(e, w2[l, o:o + FB, :]).astype(bf16).astype(f32)
                g, slope = gelu_and_slope(ub[b, :, o:o + FB])
                qq = (p * slope).astype(bf16)
                qs[:, o:o + FB] = qq
                acc1[l, :, o:o + FB] += dot(hTl, qq)
                acc2[l, :, o:o + FB] += dot(eT, g.astype(bf16))

            @pl.when(own | (l > 0))
            def _():
                dh = dot_nt(qs[...], w1[l])
                ecur[...] = (ecur[...].astype(f32) + dh).astype(bf16)

            @pl.when(own & (li == 0))
            def _():
                for p_ in range(3):
                    e_fwd(jp, p_).start()

            @pl.when(t == NSTEP - 1)
            def _():
                for cp in final_copies(l):
                    cp.start()

            return carry

        lax.fori_loop(0, NL, layer, 0)

        @pl.when(own)
        def _():
            @pl.when(k > 0)
            def _():
                eout[jp] = ecur[...]
                e_out(jp).start()

            @pl.when(jp == 1)
            def _():
                @pl.when(k == 7)
                def _():
                    for p_ in range(3):
                        l_peer(p_).start()
                    for p_ in range(3):
                        qq_ = (q + 1 + p_) % 4
                        rcopy(lmine, lbuf.at[qq_], lsend.at[p_], lrecv.at[qq_], peers[p_]).wait_recv()
                    lbuf[q] = lmine[...]
                    tot = (lbuf[0] + lbuf[1]) + (lbuf[2] + lbuf[3])
                    loss_out[...] = jnp.zeros((8, 128), f32) + jnp.sum(tot) * (0.5 * inv_total)

                @pl.when(k < 7)
                def _():
                    l_chain().wait_recv()

                @pl.when(k > 0)
                def _():
                    l_chain().start()

    half_own = pl.ds(pl.multiple_of(96 * c, 8), 96)
    half_oth = pl.ds(pl.multiple_of(96 * (1 - c), 8), 96)

    def final_copies(l):
        L = NL * c + l
        return [
            rcopy(acc1.at[l, half_oth, :], out_up.at[L], xo_s.at[l, 0], xo_r.at[l, 0], partner),
            rcopy(acc2.at[l, half_oth, :], out_down.at[L], xo_s.at[l, 1], xo_r.at[l, 1], partner),
            lcopy(acc1.at[l, half_own, :], out_up.at[L], lo_s.at[l, 0]),
            lcopy(acc2.at[l, half_own, :], out_down.at[L], lo_s.at[l, 1]),
        ]

    def step(t, carry):
        @pl.when(is_f_own(t))
        def _():
            f_own(t)

        @pl.when(is_f_oth(t))
        def _():
            f_oth(t)

        @pl.when(is_b(t))
        def _():
            b_step(t)

        return carry

    lax.fori_loop(0, NSTEP, step, 0)

    for j in range(4):
        for p in range(3):
            h_fwd(j, p).wait_send()
    for jp in range(2):
        for p in range(3):
            e_fwd(jp, p).wait_send()

    @pl.when(k < 7)
    def _():
        for j in range(4):
            h_out(j).wait_send()

    @pl.when(k > 0)
    def _():
        for jp in range(2):
            e_out(jp).wait_send()
        l_chain().wait_send()

    @pl.when(k == 1)
    def _():
        xcopy(0).wait_send()
        xcopy(1).wait_send()

    @pl.when(k == 6)
    def _():
        tcopy().wait_send()

    @pl.when(k == 7)
    def _():
        for p in range(3):
            l_peer(p).wait_send()

    for l in range(NL):
        L = NL * (1 - c) + l
        rcopy(acc1.at[l, half_oth, :], out_up.at[L], xo_s.at[l, 0], xo_r.at[l, 0], partner).wait_recv()
        rcopy(acc2.at[l, half_oth, :], out_down.at[L], xo_s.at[l, 1], xo_r.at[l, 1], partner).wait_recv()
        r1, r2, l1, l2 = final_copies(l)
        r1.wait_send()
        r2.wait_send()
        l1.wait()
        l2.wait()


def solution(mesh):
    n_data = mesh.shape["data"]

    def per_device(inputs, targets, w_up, w_down):
        n_micro, n_tok, width = inputs.shape
        inv_total = 1.0 / (n_data * n_micro * n_tok)
        x = inputs.reshape(n_micro * n_tok, width)
        y = targets.reshape(n_micro * n_tok, width)
        V = pltpu.VMEM
        DMA = pltpu.SemaphoreType.DMA
        anyspec = pl.BlockSpec(memory_space=pl.ANY)
        loss, g_up, g_down, _ = pl.pallas_call(
            functools.partial(kernel, inv_total),
            out_shape=(
                jax.ShapeDtypeStruct((8, 128), f32),
                jax.ShapeDtypeStruct((2 * NL, 96, F), f32),
                jax.ShapeDtypeStruct((2 * NL, 96, F), f32),
                jax.ShapeDtypeStruct((NL, 8, PR, F), f32),
            ),
            in_specs=[anyspec] * 4,
            out_specs=(pl.BlockSpec(memory_space=pltpu.VMEM), anyspec, anyspec, anyspec),
            scratch_shapes=[
                V((NL, D, F), bf16), V((NL, F, D), bf16),
                V((8, PR, D), bf16), V((8, PR, D), bf16),
                V((NL, DS, F), f32), V((NL, DS, F), f32),
                V((2, PR, F), f32), V((PR, F), bf16), V((PR, F), bf16),
                V((NL, 8, DS, PR), bf16), V((PR, D), bf16), V((PR, D), bf16),
                V((2, PR, D), bf16), V((2, PR, D), bf16),
                V((DS, D), bf16), V((8, 128), f32), V((4, 8, 128), f32), V((8, 128), f32),
                DMA((NL, 2)), DMA((16,)), DMA((8,)), DMA((2,)), DMA((4,)), DMA((2,)),
                DMA((4, 3)), DMA((2, 3)), DMA((4,)), DMA((2,)), DMA((1,)), DMA((3,)), DMA, DMA,
                DMA((2,)), DMA((2,)), DMA((NL, 2)), DMA((NL, 2)), DMA((NL, 2)),
            ],
            compiler_params=pltpu.CompilerParams(collective_id=0, has_side_effects=True, vmem_limit_bytes=67043328),
            name="stack_step",
        )(x, y, w_up, w_down)
        return loss[0, 0], g_up, jnp.swapaxes(g_down, 1, 2)

    return jax.shard_map(
        per_device,
        mesh=mesh,
        in_specs=(P("data", None, None), P("data", None, None), P("stage", None, None), P("stage", None, None)),
        out_specs=(P(), P("stage", "data", None), P("stage", None, "data")),
        check_vma=False,
    )
```

time: 2870 us -> 338 us (0.12)
  the two profiles are of different devices: /device:TPU:31 before, /device:TPU:5 now
where the time goes in v1:
time: 338 us
  Pallas kernels  327 us (97%)
  local copies, waits for them, and re-layouts  11.1 us (3%)
    pallas_call x1, Pallas kernels, per_device(): pl.pallas_call(functools.partial(kernel, inv_total), out_shape=(jax.Shape...  327 us
    unnamed x4, local copies, waits for them, and re-layouts  9.94 us

profile of v1, /device:TPU:5, one launch (start us, length us, event | category | flops | bytes accessed | tf_op | source)
XLA Modules:
  0.0 338.3 jit_solution(4991983563430198085)
XLA Ops:
  0.6 326.5 %stack_step.1 = (f32[8,128]{1,0:T(8,128)}, f32[6,96,3072]{2,1,0:T(8,128)}, f32[6,96,3072]{2,1,0:T(8,128)}, f32[3,8,256,3072]{3,2,1,0:T(8,128)}) custom-call(bf16[256,768]{1,0:T(8,128)(2,1)} %bitcast.5, bf16[256,768]{1,0:T(8,128)(2,1)} %bitcast.6, bf16[6,768,3072]{2,1,0:T(8,128)(2,1)} %w_up.1, bf16[6,3072,768]{2,1,0:T(8,128)(2,1)} %w_down.1), custom_call_target="tpu_custom_call" | custom-call | tf_op jit(solution)/shard_map/stack_step/pallas_call | solution.py:471
  327.2 1.2 slice.3
  328.3 0.0 copy-start
  328.3 7.0 %copy.9 = f32[6,96,3072]{2,1,0:T(8,128)} copy(f32[6,96,3072]{2,1,0:T(8,128)} %get-tuple-element.13) | data formatting | bytes 14155776
  335.3 0.0 copy-done
  335.3 3.0 copy.10
Async XLA Ops:
  328.3 7.0 %copy-start = (f32[6,96,3072]{2,1,0:T(8,128)S(1)}, f32[6,96,3072]{2,1,0:T(8,128)}, u32[]{:S(2)}) copy-start(f32[6,96,3072]{2,1,0:T(8,128)} %get-tuple-element.8) | copy-start | bytes 21233668

commit v2 on v1

v2 whole, which is shorter than its diff:
```python
import functools

import jax
import jax.numpy as jnp
from jax import lax
from jax.experimental import pallas as pl
from jax.experimental.pallas import tpu as pltpu
from jax.sharding import PartitionSpec as P

bf16, f32 = jnp.bfloat16, jnp.float32
MESH = pl.DeviceIdType.MESH
NT = (((1,), (1,)), ((), ()))
C0 = 0.7978845608028654
C1 = C0 * 0.044715
D, F = 768, 3072
CH, PR = 128, 256
NL = 3
DS = 192
FB = 768
BLOCKS = [i * FB for i in range(F // FB)]
NSTEP = 23


def nn(a, b):
    return jnp.dot(a, b, preferred_element_type=f32)


def nt(a, b):
    return lax.dot_general(a, b, NT, preferred_element_type=f32)


def gelu_and_slope(u):
    s = u * u
    t = jnp.tanh(u * (C0 + C1 * s))
    a = 1.0 + t
    g = (0.5 * u) * a
    return g, 0.5 * a + g * ((1.0 - t) * (C0 + (3.0 * C1) * s))


def kernel(inv_total, x_in, y_in, w_up, w_down,
           loss_out, out_up, out_down, s_hbm, g_hbm, q_hbm, wta, wtb, hx, ex,
           wa, wb, acc1, acc2, hs, es, sb, gb, qb, hT, eTs, hb, eb, eout, tgt, sel, ltile, lbuf, lmine,
           wsem, rsem, hrecv, erecv, trecv, lrecv, xsend, hfwd, efwd, hsend, esend, tsend, lsend, lchain_s, lchain_r,
           os_s, os_g, os_q, is_s, is_g, is_q, is_h, is_e, tr_q, tr_h, xo_s, xo_r, lo_s):
    s = lax.axis_index("stage")
    d = lax.axis_index("data")
    c = d % 2
    q = d // 2
    k = 2 * s + c
    nxt = (s + c, d + 1 - 2 * c)
    prv = (s - 1 + c, d + 1 - 2 * c)
    partner = (s, d + 1 - 2 * c)
    peers = [(s, ((q + p) % 4) * 2 + c) for p in (1, 2, 3)]

    def rcopy(src, dst, ss, rs, dev):
        return pltpu.make_async_remote_copy(src_ref=src, dst_ref=dst, send_sem=ss, recv_sem=rs, device_id=dev, device_id_type=MESH)

    lcopy = pltpu.make_async_copy

    bar = pltpu.get_barrier_semaphore()
    for dev in peers:
        pl.semaphore_signal(bar, inc=1, device_id=dev, device_id_type=MESH)

    @pl.when(k < 7)
    def _():
        pl.semaphore_signal(bar, inc=1, device_id=nxt, device_id_type=MESH)

    @pl.when(k > 0)
    def _():
        pl.semaphore_signal(bar, inc=1, device_id=prv, device_id_type=MESH)

    def w_load(l):
        return (lcopy(w_up.at[NL * c + l], wa.at[l], wsem.at[l, 0]),
                lcopy(w_down.at[NL * c + l], wb.at[l], wsem.at[l, 1]))

    def w_reload(l):
        return (lcopy(wta.at[l], wa.at[l], rsem.at[l, 0]),
                lcopy(wtb.at[l], wb.at[l], rsem.at[l, 1]))

    def start_all(cps):
        for cp in cps:
            cp.start()

    def wait_all(cps):
        for cp in cps:
            cp.wait()

    for l in range(NL):
        start_all(w_load(l))

    def half(ch):
        return pl.ds(pl.multiple_of((ch % 2) * CH, CH), CH)

    def own(ref, j):
        return ref.at[j // 2, half(j), :]

    own0 = 4 * q

    @pl.when(k == 0)
    def _():
        for j in range(2):
            lcopy(x_in.at[pl.ds(j * CH, CH), :], own(hs, j), hrecv.at[own0 + j]).start()

    @pl.when(k == 7)
    def _():
        lcopy(y_in, tgt.at[1], trecv.at[1]).start()

    row = lax.broadcasted_iota(jnp.int32, (DS, D), 0)
    col = lax.broadcasted_iota(jnp.int32, (DS, D), 1)
    sel[...] = jnp.where(col == row + DS * q, 1.0, 0.0).astype(bf16)
    ltile[...] = jnp.zeros_like(ltile)

    pl.semaphore_wait(bar, 3 + jnp.where(k < 7, 1, 0) + jnp.where(k > 0, 1, 0))

    def xcopy(j):
        return rcopy(x_in.at[pl.ds(j * CH, CH), :], own(hs, 2 + j), xsend.at[j], hrecv.at[own0 + 2 + j], partner)

    def tcopy():
        return rcopy(y_in, tgt.at[0], tsend.at[0], trecv.at[0], partner)

    @pl.when(k == 1)
    def _():
        xcopy(0).start()
        xcopy(1).start()

    @pl.when(k == 6)
    def _():
        tcopy().start()

    def h_fwd(j, p):
        ch = own0 + j
        return rcopy(own(hs, j), hx.at[ch // 2, half(ch), :], hfwd.at[j, p], hrecv.at[ch], peers[p])

    def e_fwd(j, p):
        ch = own0 + j
        return rcopy(own(es, j), ex.at[ch // 2, half(ch), :], efwd.at[j, p], erecv.at[ch], peers[p])

    def h_out(j):
        return rcopy(own(tgt, j), own(hs, j), hsend.at[j], hrecv.at[own0 + j], nxt)

    def e_out(j):
        return rcopy(own(eout, j), own(es, j), esend.at[j], erecv.at[own0 + j], prv)

    def l_peer(p):
        return rcopy(lmine, lbuf.at[q], lsend.at[p], lrecv.at[q], peers[p])

    def l_chain():
        return rcopy(loss_out, loss_out, lchain_s, lchain_r, prv)

    def wait_chunk(buf, sems, ch):
        rcopy(own(buf, 0), own(buf, 0), hfwd.at[0, 0], sems.at[ch], peers[0]).wait_recv()

    def s_out_own(l, ch, b):
        return lcopy(sb.at[b, pl.ds(0, CH), :], s_hbm.at[l, ch // 2, half(ch), :], os_s.at[b])

    def g_out_own(l, ch, b):
        return lcopy(gb.at[b, pl.ds(0, CH), :], g_hbm.at[l, ch // 2, half(ch), :], os_g.at[b])

    def q_out_own(l, j, b):
        return lcopy(qb.at[b, pl.ds(0, CH), :], q_hbm.at[l, j // 2, half(j), :], os_q.at[b])

    def f_outs(l, pr, b):
        return lcopy(sb.at[b], s_hbm.at[l, pr], os_s.at[b]), lcopy(gb.at[b], g_hbm.at[l, pr], os_g.at[b])

    def s_in_own(l, ch, b):
        return lcopy(s_hbm.at[l, ch // 2, half(ch), :], sb.at[b, pl.ds(0, CH), :], is_s.at[b])

    def b_ins(l, pr, b):
        return lcopy(s_hbm.at[l, pr], sb.at[b], is_s.at[b]), lcopy(g_hbm.at[l, pr], gb.at[b], is_g.at[b])

    def w_ins(l, jp, b):
        return lcopy(q_hbm.at[l, jp], qb.at[b], is_q.at[b]), lcopy(g_hbm.at[l, 2 * q + jp], gb.at[b], is_g.at[b])

    def h_in(pr, b):
        return lcopy(hx.at[pr], hb.at[b], is_h.at[b])

    def e_in(pr, b):
        return lcopy(ex.at[pr], eb.at[b], is_e.at[b])

    high = k >= 4
    m = jnp.minimum(6, 2 * (7 - k))

    def is_tr(t):
        return t == jnp.where(high, 0, 4)

    def f_own_j(t):
        return jnp.where(high, t - 1, t)

    def is_f_own(t):
        return (t < 5) & jnp.logical_not(is_tr(t))

    def is_b_own(t):
        return (t >= 5 + m) & (t < 9 + m)

    def b_own_j(t):
        return t - 5 - m

    def is_w(t):
        return (t >= 9 + m) & (t < 11 + m)

    def w_jp(t):
        return t - 9 - m

    def is_b_oth(t):
        return (t >= 17) & (t < NSTEP)

    def is_f_oth(t):
        return ((t >= 5) & (t < 5 + m)) | ((t >= 11 + m) & (t < 17))

    def oth_pair(i):
        return 2 * ((q + 1 + i % 3) % 4) + i // 3

    def f_pair(t):
        return oth_pair(jnp.where(t < 5 + m, t - 5, t - 11))

    def b_pair(t):
        return oth_pair(t - 17)

    def is_loader(t):
        return is_b_own(t) | is_w(t) | is_b_oth(t)

    def start_load(t, li, b):
        l = 2 - li

        @pl.when(is_b_own(t))
        def _():
            s_in_own(l, own0 + b_own_j(t), b).start()

        @pl.when(is_w(t))
        def _():
            start_all(w_ins(l, w_jp(t), b))

        @pl.when(is_b_oth(t))
        def _():
            start_all(b_ins(l, b_pair(t), b))

    def next_load(t, li, b):
        @pl.when(li < 2)
        def _():
            start_load(t, li + 1, 1 - b)

        @pl.when(li == 2)
        def _():
            start_load(t + 1, 0, 1 - b)

    def first_load(t):
        @pl.when(is_f_oth(t - 1))
        def _():
            wait_all(f_outs(2, 0, (t + 1) % 2))

        @pl.when(jnp.logical_not(is_loader(t - 1)))
        def _():
            start_load(t, 0, t % 2)

    def pre_h(t):
        @pl.when(is_f_oth(t + 1))
        def _():
            pr = f_pair(t + 1)
            wait_chunk(hs, hrecv, 2 * pr)
            wait_chunk(hs, hrecv, 2 * pr + 1)
            h_in(pr, (t + 1) % 2).start()

    def pre_e(t):
        @pl.when(is_b_oth(t + 1))
        def _():
            pr = b_pair(t + 1)
            wait_chunk(es, erecv, 2 * pr)
            wait_chunk(es, erecv, 2 * pr + 1)
            e_in(pr, (t + 1) % 2).start()

    def wait_reload(t, l):
        @pl.when(t == 5)
        def _():
            wait_all(w_reload(l))

    def tr_step(t):
        def zero(i, carry):
            r = pl.ds(pl.multiple_of(i * 8, 8), 8)
            for l in range(NL):
                acc1[l, r, :] = jnp.zeros((8, F), f32)
                acc2[l, r, :] = jnp.zeros((8, F), f32)
            return carry

        lax.fori_loop(0, DS // 8, zero, 0)

        def layer(l, carry):
            @pl.when(high)
            def _():
                wait_all(w_load(l))

            stage = [hb.at[0], hb.at[1], eb.at[0], eb.at[1]]
            pend_q, pend_h = [None] * 2, [None] * 4
            for i in range(3):
                if pend_q[i % 2] is not None:
                    pend_q[i % 2].wait()
                qb[i % 2] = wb[l, :, i * 256:(i + 1) * 256].T
                pend_q[i % 2] = lcopy(qb.at[i % 2], wta.at[l, pl.ds(i * 256, 256), :], tr_q.at[i % 2])
                pend_q[i % 2].start()
                for r in range(4 * i, 4 * i + 4):
                    if pend_h[r % 4] is not None:
                        pend_h[r % 4].wait()
                    stage[r % 4][...] = wa[l, :, r * 256:(r + 1) * 256].T
                    pend_h[r % 4] = lcopy(stage[r % 4], wtb.at[l, pl.ds(r * 256, 256), :], tr_h.at[r % 4])
                    pend_h[r % 4].start()
            wait_all(pend_q + pend_h)

            @pl.when(jnp.logical_not(high))
            def _():
                start_all(w_reload(l))

            return carry

        lax.fori_loop(0, NL, layer, 0)
        pre_h(t)

    def f_own(t):
        j = f_own_j(t)
        ch = own0 + j
        wait_chunk(hs, hrecv, ch)
        for p in range(3):
            h_fwd(j, p).start()
        pre_h(t)
        hb[0, 0:CH, :] = hs[j // 2, half(j), :]

        def layer(l, carry):
            b = l % 2

            @pl.when((j == 0) & jnp.logical_not(high))
            def _():
                wait_all(w_load(l))

            @pl.when(l == 2)
            def _():
                s_out_own(0, ch, 0).wait()
                g_out_own(0, ch, 0).wait()

            h = hb[0, 0:CH, :]
            hT[l, ch // 2, :, half(ch)] = nt(sel[...], h).astype(bf16)
            for o in BLOCKS:
                g, slope = gelu_and_slope(nn(h, wa[l, :, o:o + FB]))
                sb[b, 0:CH, o:o + FB] = slope
                gb[b, 0:CH, o:o + FB] = g.astype(bf16)
            hb[0, 0:CH, :] = (h.astype(f32) + nn(gb[b, 0:CH, :], wb[l])).astype(bf16)
            s_out_own(l, ch, b).start()
            g_out_own(l, ch, b).start()

            @pl.when((j == 3) & high)
            def _():
                start_all(w_reload(l))

            return carry

        lax.fori_loop(0, NL, layer, 0)

        @pl.when(k < 7)
        def _():
            tgt[j // 2, half(j), :] = hb[0, 0:CH, :]
            h_out(j).start()

        @pl.when(k == 7)
        def _():
            @pl.when(j == 0)
            def _():
                rcopy(y_in, tgt.at[0], tsend.at[0], trecv.at[0], partner).wait_recv()

            @pl.when(j == 2)
            def _():
                lcopy(y_in, tgt.at[1], trecv.at[1]).wait()

            diff = hb[0, 0:CH, :].astype(f32) - tgt[j // 2, half(j), :].astype(f32)
            es[j // 2, half(j), :] = (diff * inv_total).astype(bf16)
            sq = jnp.sum((diff * diff).reshape(CH // 8, 8, D), axis=0)
            ltile[...] += sum(sq[:, i * 128:(i + 1) * 128] for i in range(D // 128))

            @pl.when(j == 3)
            def _():
                lmine[...] = ltile[...]

        s_out_own(1, ch, 1).wait()
        g_out_own(1, ch, 1).wait()
        s_out_own(2, ch, 0).wait()
        g_out_own(2, ch, 0).wait()

    def f_oth(t):
        pr = f_pair(t)
        hi = t % 2
        h_in(pr, hi).wait()

        def layer(l, carry):
            b = (t + l) % 2
            wait_reload(t, l)

            @pl.when((l == 1) & is_f_oth(t - 1))
            def _():
                wait_all(f_outs(2, 0, b))

            @pl.when(l == 1)
            def _():
                pre_h(t)
                pre_e(t)

            @pl.when(l == 2)
            def _():
                wait_all(f_outs(0, pr, b))

            h = hb[hi]
            hT[l, pr] = nt(sel[...], h).astype(bf16)
            for o in BLOCKS:
                g, slope = gelu_and_slope(nt(h, wb[l, o:o + FB, :]))
                sb[b, :, o:o + FB] = slope
                gb[b, :, o:o + FB] = g.astype(bf16)
            start_all(f_outs(l, pr, b))

            @pl.when(l < 2)
            def _():
                hb[hi] = (hb[hi].astype(f32) + nt(gb[b], wa[l])).astype(bf16)

            return carry

        lax.fori_loop(0, NL, layer, 0)
        wait_all(f_outs(1, pr, (t + 1) % 2))

    def b_own(t):
        j = b_own_j(t)
        ch = own0 + j
        jp = j // 2
        first_load(t)

        @pl.when(k < 7)
        def _():
            wait_chunk(es, erecv, ch)

        for p in range(3):
            e_fwd(j, p).start()
        eb[0, 0:CH, :] = es[jp, half(j), :]

        def layer(li, carry):
            l = 2 - li
            b = (t + li) % 2
            s_in_own(l, ch, b).wait()

            @pl.when(li == 2)
            def _():
                q_out_own(2, j, b).wait()
                q_out_own(1, j, 1 - b).wait()

            next_load(t, li, b)
            wait_reload(t, l)
            e = eb[0, 0:CH, :]
            eTs[jp, l, :, half(j)] = nt(sel[...], e).astype(bf16)
            for o in BLOCKS:
                p = nn(e, wa[l, :, o:o + FB]).astype(bf16).astype(f32)
                qb[b, 0:CH, o:o + FB] = (p * sb[b, 0:CH, o:o + FB]).astype(bf16)
            eb[0, 0:CH, :] = (e.astype(f32) + nn(qb[b, 0:CH, :], wb[l])).astype(bf16)
            q_out_own(l, j, b).start()
            return carry

        lax.fori_loop(0, NL, layer, 0)

        @pl.when(k > 0)
        def _():
            eout[jp, half(j), :] = eb[0, 0:CH, :]
            e_out(j).start()

        q_out_own(0, j, t % 2).wait()

    def wgrad(l, hTl, eTl, b):
        for o in BLOCKS:
            acc1[l, :, o:o + FB] += nn(hTl, qb[b, :, o:o + FB])
            acc2[l, :, o:o + FB] += nn(eTl, gb[b, :, o:o + FB])

    def w_step(t):
        jp = w_jp(t)

        def layer(li, carry):
            l = 2 - li
            b = (t + li) % 2
            wait_all(w_ins(l, jp, b))
            next_load(t, li, b)

            @pl.when(li == 1)
            def _():
                pre_h(t)
                pre_e(t)

            wgrad(l, hT[l, 2 * q + jp], eTs[jp, l], b)
            return carry

        lax.fori_loop(0, NL, layer, 0)

        @pl.when(jp == 1)
        def _():
            @pl.when(k == 7)
            def _():
                for p in range(3):
                    l_peer(p).start()
                for p in range(3):
                    qo = (q + 1 + p) % 4
                    rcopy(lmine, lbuf.at[qo], lsend.at[p], lrecv.at[qo], peers[p]).wait_recv()
                lbuf[q] = lmine[...]
                tot = (lbuf[0] + lbuf[1]) + (lbuf[2] + lbuf[3])
                loss_out[...] = jnp.zeros((8, 128), f32) + jnp.sum(tot) * (0.5 * inv_total)

            @pl.when(k < 7)
            def _():
                l_chain().wait_recv()

            @pl.when(k > 0)
            def _():
                l_chain().start()

    half_own = pl.ds(pl.multiple_of(96 * c, 8), 96)
    half_oth = pl.ds(pl.multiple_of(96 * (1 - c), 8), 96)

    def final_copies(l):
        lg = NL * c + l
        return [
            rcopy(acc1.at[l, half_oth, :], out_up.at[lg], xo_s.at[l, 0], xo_r.at[l, 0], partner),
            rcopy(acc2.at[l, half_oth, :], out_down.at[lg], xo_s.at[l, 1], xo_r.at[l, 1], partner),
            lcopy(acc1.at[l, half_own, :], out_up.at[lg], lo_s.at[l, 0]),
            lcopy(acc2.at[l, half_own, :], out_down.at[lg], lo_s.at[l, 1]),
        ]

    def b_oth(t):
        pr = b_pair(t)
        ei = t % 2
        first_load(t)
        e_in(pr, ei).wait()

        def layer(li, carry):
            l = 2 - li
            b = (t + li) % 2
            wait_all(b_ins(l, pr, b))
            next_load(t, li, b)

            @pl.when(li == 1)
            def _():
                pre_e(t)

            e = eb[ei]
            eT = nt(sel[...], e).astype(bf16)
            for o in BLOCKS:
                p = nn(e, wa[l, :, o:o + FB]).astype(bf16).astype(f32)
                qb[b, :, o:o + FB] = (p * sb[b, :, o:o + FB]).astype(bf16)
            wgrad(l, hT[l, pr], eT, b)

            @pl.when(l > 0)
            def _():
                eb[ei] = (eb[ei].astype(f32) + nn(qb[b], wb[l])).astype(bf16)

            @pl.when(t == NSTEP - 1)
            def _():
                start_all(final_copies(l))

            return carry

        lax.fori_loop(0, NL, layer, 0)

    def step(t, carry):
        for test, run in ((is_tr, tr_step), (is_f_own, f_own), (is_f_oth, f_oth), (is_b_own, b_own), (is_w, w_step), (is_b_oth, b_oth)):
            @pl.when(test(t))
            def _():
                run(t)

        return carry

    lax.fori_loop(0, NSTEP, step, 0)

    for j in range(4):
        for p in range(3):
            h_fwd(j, p).wait_send()
            e_fwd(j, p).wait_send()

    @pl.when(k < 7)
    def _():
        for j in range(4):
            h_out(j).wait_send()

    @pl.when(k > 0)
    def _():
        for j in range(4):
            e_out(j).wait_send()
        l_chain().wait_send()

    @pl.when(k == 1)
    def _():
        xcopy(0).wait_send()
        xcopy(1).wait_send()

    @pl.when(k == 6)
    def _():
        tcopy().wait_send()

    @pl.when(k == 7)
    def _():
        for p in range(3):
            l_peer(p).wait_send()

    for l in range(NL):
        lg = NL * (1 - c) + l
        rcopy(acc1.at[l, half_oth, :], out_up.at[lg], xo_s.at[l, 0], xo_r.at[l, 0], partner).wait_recv()
        rcopy(acc2.at[l, half_oth, :], out_down.at[lg], xo_s.at[l, 1], xo_r.at[l, 1], partner).wait_recv()
        r1, r2, l1, l2 = final_copies(l)
        r1.wait_send()
        r2.wait_send()
        l1.wait()
        l2.wait()


def solution(mesh):
    n_data = mesh.shape["data"]

    def per_device(inputs, targets, w_up, w_down):
        n_micro, n_tok, width = inputs.shape
        inv_total = 1.0 / (n_data * n_micro * n_tok)
        x = inputs.reshape(n_micro * n_tok, width)
        y = targets.reshape(n_micro * n_tok, width)
        V = pltpu.VMEM
        DMA = pltpu.SemaphoreType.DMA
        S = jax.ShapeDtypeStruct
        anyspec = pl.BlockSpec(memory_space=pl.ANY)
        outs = pl.pallas_call(
            functools.partial(kernel, inv_total),
            out_shape=(
                S((8, 128), f32), S((2 * NL, 96, F), f32), S((2 * NL, 96, F), f32),
                S((NL, 8, PR, F), f32), S((NL, 8, PR, F), bf16), S((NL, 2, PR, F), bf16),
                S((NL, D, F), bf16), S((NL, F, D), bf16), S((8, PR, D), bf16), S((8, PR, D), bf16),
            ),
            in_specs=[anyspec] * 4,
            out_specs=(pl.BlockSpec(memory_space=pltpu.VMEM),) + (anyspec,) * 9,
            scratch_shapes=[
                V((NL, D, F), bf16), V((NL, F, D), bf16),
                V((NL, DS, F), f32), V((NL, DS, F), f32),
                V((2, PR, D), bf16), V((2, PR, D), bf16),
                V((2, PR, F), f32), V((2, PR, F), bf16), V((2, PR, F), bf16),
                V((NL, 8, DS, PR), bf16), V((2, NL, DS, PR), bf16),
                V((2, PR, D), bf16), V((2, PR, D), bf16), V((2, PR, D), bf16), V((2, PR, D), bf16),
                V((DS, D), bf16), V((8, 128), f32), V((4, 8, 128), f32), V((8, 128), f32),
                DMA((NL, 2)), DMA((NL, 2)), DMA((16,)), DMA((16,)), DMA((2,)), DMA((4,)), DMA((2,)),
                DMA((4, 3)), DMA((4, 3)), DMA((4,)), DMA((4,)), DMA((1,)), DMA((3,)), DMA, DMA,
                DMA((2,)), DMA((2,)), DMA((2,)), DMA((2,)), DMA((2,)), DMA((2,)), DMA((2,)), DMA((2,)), DMA((2,)), DMA((4,)),
                DMA((NL, 2)), DMA((NL, 2)), DMA((NL, 2)),
            ],
            compiler_params=pltpu.CompilerParams(collective_id=0, has_side_effects=True, vmem_limit_bytes=67043328),
            name="stack_step",
        )(x, y, w_up, w_down)
        return outs[0][0, 0], outs[1], jnp.swapaxes(outs[2], 1, 2)

    return jax.shard_map(
        per_device,
        mesh=mesh,
        in_specs=(P("data", None, None), P("data", None, None), P("stage", None, None), P("stage", None, None)),
        out_specs=(P(), P("stage", "data", None), P("stage", None, "data")),
        check_vma=False,
    )
```

time: 338 us -> 275 us (0.81)
  the two profiles are of different devices: /device:TPU:5 before, /device:TPU:31 now
where the time goes in v2:
time: 275 us; the launch traced here: 273 us
  Pallas kernels  261 us (95%)
  local copies, waits for them, and re-layouts  11.3 us (4%)
    pallas_call x1, Pallas kernels, per_device(): pl.pallas_call(functools.partial(kernel, inv_total), out_shape=(S((8, 128...  261 us
    unnamed x6, local copies, waits for them, and re-layouts  9.94 us

profile of v2, /device:TPU:31, one launch (start us, length us, event | category | flops | bytes accessed | tf_op | source)
XLA Modules:
  0.0 273.1 jit_solution(12036293289969711260)
XLA Ops:
  0.6 261.2 %stack_step.1 = (f32[8,128]{1,0:T(8,128)}, f32[6,96,3072]{2,1,0:T(8,128)}, f32[6,96,3072]{2,1,0:T(8,128)}, f32[3,8,256,3072]{3,2,1,0:T(8,128)}, bf16[3,8,256,307...) custom-call(bf16[256,768]{1,0:T(8,128)(2,1)} %bitcast.7, ...), custom_call_target="tpu_custom_call" | custom-call | tf_op jit(solution)/shard_map/stack_step/pallas_call | solution.py:622
  261.9 0.0 slice-start
  261.9 1.3 slice.3
  263.2 0.0 slice-start.1
  263.2 7.0 %copy.9 = f32[6,96,3072]{2,1,0:T(8,128)} copy(f32[6,96,3072]{2,1,0:T(8,128)} %get-tuple-element.13) | data formatting | bytes 14155776
  270.2 0.0 slice-done
  270.2 0.0 slice-done.1
  270.2 3.0 %copy.10 = f32[6,3072,96]{1,2,0:T(8,128)} copy(f32[6,3072,96]{1,2,0:T(8,128)S(1)} %bitcast.6) | data formatting | bytes 14155776
  (1 shorter events, 0.0 us)
Async XLA Ops:
  261.9 8.3 %slice-start = ((s8[7077888]{0:T(1024)(128)(4,1)}), s8[4194304]{0:T(1024)(128)(4,1)S(1)}, s32[]{:S(2)}) async-start(s8[7077888]{0:T(1024)(128)(4,1)} %bitcast.4), calls=%async_computation | async-start | bytes 8388608
  263.2 7.0 %slice-start.1 = ((s8[7077888]{0:T(1024)(128)(4,1)}), s8[2883584]{0:T(1024)(128)(4,1)S(1)}, s32[]{:S(2)}) async-start(s8[7077888]{0:T(1024)(128)(4,1)} %bitcast.4), calls=%async_computation.1 | async-start | bytes 5767168

commit v3 on v2

v3 whole, which is shorter than its diff:
```python
import functools

import jax
import jax.numpy as jnp
from jax import lax
from jax.experimental import pallas as pl
from jax.experimental.pallas import tpu as pltpu
from jax.sharding import PartitionSpec as P

bf16, f32 = jnp.bfloat16, jnp.float32
MESH = pl.DeviceIdType.MESH
NT = (((1,), (1,)), ((), ()))
C0 = 0.7978845608028654
C1 = C0 * 0.044715
D, F = 768, 3072
CH, PR = 128, 256
NL = 3
DS = 192
FB, FW, DW = 512, 768, 256
BLOCKS = [i * FB for i in range(F // FB)]
NSTEP = 23
PER = 2
TOP = NL - 1
PEERS = range(3)
HEAD = slice(0, CH)


def each_layer(layer, peel=False):
    if peel:
        layer(0, 0)
    lax.fori_loop(int(peel), NL, layer, 0)


def flip(t):
    return (t + 1) % PER


def nn(a, b):
    return jnp.dot(a, b, preferred_element_type=f32)


def nt(a, b):
    return lax.dot_general(a, b, NT, preferred_element_type=f32)


def gelu_and_slope(u):
    s = u * u
    t = jnp.tanh(u * (C0 + C1 * s))
    a = 1.0 + t
    g = (0.5 * u) * a
    return g, 0.5 * a + g * ((1.0 - t) * (C0 + (3.0 * C1) * s))


def two_matmuls(va, first, second):
    v = first(BLOCKS[0])
    for o in BLOCKS[1:]:
        w = first(o)
        va[...] += second(o - FB, v)
        v = w
    return va[...] + second(BLOCKS[-1], v)


def kernel(inv_total, x_in, y_in, w_up, w_down,
           loss_out, out_up, out_down, s_hbm, g_hbm, q_hbm, wta, wtb, hx, ex, hx2, ex1,
           wa, wb, acc1, acc2, hs, es, sb, gb, qb, hT, eTs, hb, eb, eout, tgt, sv, va, sel, ltile, lbuf, lmine,
           wsem, rsem, h2recv, e1recv, h2fwd, e1fwd, is_x, os_x, hrecv, erecv, trecv, lrecv, xsend, hfwd, efwd, hsend, esend, tsend, lsend, lout_s, lout_r,
           os_s, os_g, os_q, is_s, is_g, is_q, is_h, is_e, tr_q, tr_h, xo_s, xo_r, lo_s):
    s = lax.axis_index("stage")
    d = lax.axis_index("data")
    c = d % PER
    q = d // PER
    k = PER * s + c
    nxt = (s + c, d + 1 - PER * c)
    prv = (s - 1 + c, d + 1 - PER * c)
    partner = (s, d + 1 - PER * c)
    peers = [(s, ((q + p) % 4) * 2 + c) for p in (1, 2, 3)]

    def rcopy(src, dst, ss, rs, dev):
        return pltpu.make_async_remote_copy(src_ref=src, dst_ref=dst, send_sem=ss, recv_sem=rs, device_id=dev, device_id_type=MESH)

    lcopy = pltpu.make_async_copy
    hc = hb.at[0, HEAD, :]
    ec = eb.at[0, HEAD, :]

    bar = pltpu.get_barrier_semaphore()
    for dev in peers:
        pl.semaphore_signal(bar, inc=1, device_id=dev, device_id_type=MESH)

    @pl.when(k < 7)
    def _():
        pl.semaphore_signal(bar, inc=1, device_id=nxt, device_id_type=MESH)

    @pl.when(k > 0)
    def _():
        pl.semaphore_signal(bar, inc=1, device_id=prv, device_id_type=MESH)

    @pl.when(k < 6)
    def _():
        pl.semaphore_signal(bar, inc=1, device_id=(3, PER * q + 1), device_id_type=MESH)

    def w_load(l):
        return (lcopy(w_up.at[NL * c + l], wa.at[l], wsem.at[l, 0]),
                lcopy(w_down.at[NL * c + l], wb.at[l], wsem.at[l, 1]))

    def w_reload(l):
        return (lcopy(wta.at[l], wa.at[l], rsem.at[l, 0]),
                lcopy(wtb.at[l], wb.at[l], rsem.at[l, 1]))

    def start_all(cps):
        for cp in cps:
            cp.start()

    def wait_all(cps):
        for cp in cps:
            cp.wait()

    def half(ch):
        return pl.ds(pl.multiple_of((ch % PER) * CH, CH), CH)

    def own(ref, j):
        return ref.at[j // PER, half(j), :]

    own0 = 4 * q

    @pl.when(k == 0)
    def _():
        for j in range(2):
            lcopy(x_in.at[pl.ds(j * CH, CH), :], own(hs, j), hrecv.at[own0 + j]).start()

    for l in range(NL):
        start_all(w_load(l))

    @pl.when(k == 7)
    def _():
        lcopy(y_in, tgt.at[1], trecv.at[1]).start()

    row = lax.broadcasted_iota(jnp.int32, (DS, D), 0)
    col = lax.broadcasted_iota(jnp.int32, (DS, D), 1)
    sel[...] = jnp.where(col == row + DS * q, 1.0, 0.0).astype(bf16)
    ltile[...] = jnp.zeros_like(ltile)

    pl.semaphore_wait(bar, 3 + jnp.where(k < 7, 1, 7) + jnp.where((k > 0) & (k < 7), 1, 0))

    def xcopy(j):
        return rcopy(x_in.at[pl.ds(j * CH, CH), :], own(hs, 2 + j), xsend.at[j], hrecv.at[own0 + 2 + j], partner)

    def tcopy():
        return rcopy(y_in, tgt.at[0], tsend.at[0], trecv.at[0], partner)

    @pl.when(k == 1)
    def _():
        xcopy(0).start()
        xcopy(1).start()

    @pl.when(k == 6)
    def _():
        tcopy().start()

    def h_fwd(j, p):
        ch = own0 + j
        return rcopy(own(hs, j), hx.at[ch // PER, half(ch), :], hfwd.at[j, p], hrecv.at[ch], peers[p])

    def e_fwd(j, p):
        ch = own0 + j
        return rcopy(own(es, j), ex.at[ch // PER, half(ch), :], efwd.at[j, p], erecv.at[ch], peers[p])

    def h2_fwd(j, p):
        ch = own0 + j
        at = hx2.at[ch // PER, half(ch), :]
        return rcopy(at, at, h2fwd.at[j, p], h2recv.at[ch], peers[p])

    def e1_fwd(j, p):
        ch = own0 + j
        at = ex1.at[ch // PER, half(ch), :]
        return rcopy(at, at, e1fwd.at[j, p], e1recv.at[ch], peers[p])

    def h2_save(j):
        ch = own0 + j
        return lcopy(sv.at[1], hx2.at[ch // PER, half(ch), :], os_x.at[0])

    def e1_save(j, b):
        ch = own0 + j
        return lcopy(sv.at[b], ex1.at[ch // PER, half(ch), :], os_x.at[b])

    def h_out(j):
        return rcopy(own(tgt, j), own(hs, j), hsend.at[j], hrecv.at[own0 + j], nxt)

    def e_out(j):
        return rcopy(eout.at[half(j), :], own(es, j), esend.at[j], erecv.at[own0 + j], prv)

    def l_peer(p):
        return rcopy(lmine, lbuf.at[q], lsend.at[p], lrecv.at[q], peers[p])

    def l_out(kk):
        return rcopy(loss_out, loss_out, lout_s.at[kk], lout_r, (kk // PER, PER * q + kk % PER))

    def wait_chunk(buf, sems, ch):
        rcopy(own(buf, 0), own(buf, 0), hfwd.at[0, 0], sems.at[ch], peers[0]).wait_recv()

    def s_out_own(l, ch, b):
        return lcopy(sb.at[b, half(ch), :], s_hbm.at[l, ch // PER, half(ch), :], os_s.at[b])

    def g_out_own(l, ch, b):
        return lcopy(gb.at[b, half(ch), :], g_hbm.at[l, ch // PER, half(ch), :], os_g.at[b])

    def q_out_own(l, j, b):
        return lcopy(qb.at[b, HEAD, :], q_hbm.at[l, j // PER, half(j), :], os_q.at[b])

    def f_drain(b):
        s_out_own(0, 0, b).wait()
        g_out_own(0, 0, b).wait()

    def f_drain_all():
        for b in range(PER):
            f_drain(b)

    def f_outs(l, pr, b):
        return lcopy(sb.at[b], s_hbm.at[l, pr], os_s.at[b]), lcopy(gb.at[b], g_hbm.at[l, pr], os_g.at[b])

    def s_in_own(l, ch, b):
        return lcopy(s_hbm.at[l, ch // PER, half(ch), :], sb.at[b, HEAD, :], is_s.at[b])

    def b_ins(l, pr, b):
        return lcopy(s_hbm.at[l, pr], sb.at[b], is_s.at[b]), lcopy(g_hbm.at[l, pr], gb.at[b], is_g.at[b])

    def w_ins(l, jp, b):
        return lcopy(q_hbm.at[l, jp], qb.at[b], is_q.at[b]), lcopy(g_hbm.at[l, PER * q + jp], gb.at[b], is_g.at[b])

    def h_in(pr, b):
        return lcopy(hx.at[pr], hb.at[b], is_h.at[b])

    def e_in(pr, b):
        return lcopy(ex.at[pr], eb.at[b], is_e.at[b])

    def h2_in(pr, b):
        return lcopy(hx2.at[pr], tgt.at[b], is_x.at[b])

    def e1_in(pr, b):
        return lcopy(ex1.at[pr], tgt.at[b], is_x.at[b])

    def wait_pair(sems, pr):
        wait_chunk(hs, sems, PER * pr)
        wait_chunk(hs, sems, PER * pr + 1)

    first, last = k == 0, k == 7
    mid = (k > 0) & (k < 7)
    high = k >= 4

    def flag(x):
        return jnp.where(x, 1, 0)

    m = 6 * flag(k < 3) + 4 * flag(k == 3) + 3 * flag(k == 4) + 2 * flag(k == 5)
    end = jnp.where(mid, 22, 18)

    def within(t, a, b):
        return (t >= a) & (t < b)

    def is_tr(t):
        return t == jnp.where(high, 0, 4)

    def is_bx(t):
        return last & ((t == 3) | (t == 6))

    def bx_jp(t):
        return t // 6

    def is_f_own(t):
        return within(t, 0, jnp.where(last, 6, 5)) & jnp.logical_not(is_tr(t) | is_bx(t))

    def f_own_j(t):
        return jnp.where(high, t - 1, t) - flag(last & (t > 3))

    def is_b_own(t):
        return mid & (within(t, 5 + m, 7 + m) | within(t, 8 + m, 10 + m))

    def b_own_j(t):
        return t - 5 - m - flag(t > 7 + m)

    def is_w(t):
        return mid & (within(t, jnp.where(high, 15, 10 + m), jnp.where(high, 17, 11 + m)) | (is_gap(t) & jnp.logical_not(high)))

    def w_jp(t):
        return jnp.where(high, t - 15, flag(t > 7 + m))

    def is_ob(t):
        return first & ((t == 11) | (t == 14))

    def ob_jp(t):
        return t // 14

    def is_gap(t):
        return mid & (t == 7 + m)

    def is_b_oth(t):
        return (mid & within(t, 17, 23)) | (first & within(t, 11, 19)) | (last & within(t, 13, 19))

    def is_f_oth(t):
        return (first & within(t, 5, 11)) | (last & within(t, 7, 13)) | (is_gap(t) & high) | (mid & (within(t, 5, 5 + m) | within(t, jnp.where(high, 10, 11) + m, jnp.where(high, 15, 17))))

    def oth_pair(i):
        return 2 * ((q + 1 + i % 3) % 4) + i // 3

    def f_pair(t):
        i = jnp.where(t < 5 + m, t - 5, jnp.where(is_gap(t), m, jnp.where(high, t - 9, t - 11)))
        return oth_pair(jnp.where(last, t - 7, i))

    def b_pair(t):
        i0 = jnp.where(t < 14, t - 12, t - 13)
        i = jnp.where(first, i0, jnp.where(last, t - 13, t - 17))
        return jnp.where(is_ob(t), PER * q + ob_jp(t), oth_pair(jnp.maximum(i, 0)))

    def is_loader(t):
        return is_b_own(t) | is_w(t) | is_b_oth(t)

    def start_load(t, li, b):
        l = TOP - li

        @pl.when(is_b_own(t))
        def _():
            s_in_own(l, own0 + b_own_j(t), b).start()

        @pl.when(is_w(t))
        def _():
            start_all(w_ins(l, w_jp(t), b))

        @pl.when(is_b_oth(t))
        def _():
            start_all(b_ins(l, b_pair(t), b))

    def next_load(t, li, b):
        @pl.when(li < 2)
        def _():
            start_load(t, li + 1, 1 - b)

        @pl.when(li == TOP)
        def _():
            start_load(t + 1, 0, 1 - b)

    def first_load(t):
        @pl.when(is_f_oth(t - 1))
        def _():
            wait_all(f_outs(2, 0, flip(t)))

        @pl.when(is_f_own(t - 1))
        def _():
            f_drain_all()

        @pl.when(jnp.logical_not(is_loader(t - 1) | is_f_oth(t - 1) | is_f_own(t - 1)))
        def _():
            start_load(t, 0, t % PER)

    def pre_h(t):
        @pl.when(is_f_oth(t + 1))
        def _():
            pr = f_pair(t + 1)
            wait_chunk(hs, hrecv, PER * pr)
            wait_chunk(hs, hrecv, PER * pr + 1)
            h_in(pr, flip(t)).start()

    def pre_e(t):
        @pl.when(is_b_oth(t + 1) & jnp.logical_not(is_ob(t + 1)))
        def _():
            pr = b_pair(t + 1)
            wait_chunk(es, erecv, PER * pr)
            wait_chunk(es, erecv, PER * pr + 1)
            e_in(pr, flip(t)).start()

    def wait_reload(t, l):
        @pl.when(t == jnp.where(last, 7, 5))
        def _():
            wait_all(w_reload(l))

    def tr_step(t):
        def zero(i, carry):
            r = pl.ds(pl.multiple_of(i * 8, 8), 8)
            for l in range(NL):
                acc1[l, r, :] = jnp.zeros((8, F), f32)
                acc2[l, r, :] = jnp.zeros((8, F), f32)
            return carry

        lax.fori_loop(0, DS // 8, zero, 0)

        @pl.when(jnp.logical_not(high))
        def _():
            f_drain_all()

        stage = [hb.at[0], hb.at[1], eb.at[0], eb.at[1], eout]
        pend_q, pend_h = [None] * 2, [None] * 5

        def reload(l):
            @pl.when(jnp.logical_not(high))
            def _():
                start_all(w_reload(l))

        def put(pend, sems, n, buf, src, dst):
            if pend[n] is not None:
                pend[n].wait()
            for o in range(0, src.shape[0], D):
                buf[:, o:o + D] = src[o:o + D, :].T
            pend[n] = lcopy(buf, dst, sems.at[n])
            pend[n].start()

        for l in range(NL):
            @pl.when(high)
            def _():
                wait_all(w_load(l))

            for i in range(3):
                put(pend_q, tr_q, i % PER, qb.at[i % PER], wb.at[l, :, pl.ds(i * 256, 256)], wta.at[l, pl.ds(i * 256, 256), :])
                for r in range(4 * i, 4 * i + 4):
                    put(pend_h, tr_h, r % 5, stage[r % 5], wa.at[l, :, pl.ds(r * 256, 256)], wtb.at[l, pl.ds(r * 256, 256), :])
            if l > 0:
                reload(l - 1)
        wait_all(pend_q + pend_h)
        reload(NL - 1)
        pre_h(t)

    def f_own(t):
        j = f_own_j(t)
        ch = own0 + j
        rows = half(j)
        wait_chunk(hs, hrecv, ch)
        for p in PEERS:
            h_fwd(j, p).start()
        hc[...] = hs[j // PER, rows, :]

        def layer(l, carry):
            b = l % PER

            @pl.when((j == 0) & jnp.logical_not(high))
            def _():
                wait_all(w_load(l))

            @pl.when((l == TOP) | is_f_own(t - 1))
            def _():
                f_drain(b)

            @pl.when((k == 6) & (j == 3) & (l == 1))
            def _():
                start_load(t + 1, 0, flip(t))

            h = hc[...]

            sv[jnp.maximum(l - 1, 0)] = h
            acc = va.at[HEAD, :]
            acc[...] = h.astype(f32)

            def up(o):
                g, slope = gelu_and_slope(nn(h, wa[l, :, o:o + FB]))
                sb[b, rows, o:o + FB] = slope
                g = g.astype(bf16)
                gb[b, rows, o:o + FB] = g
                return g

            hc[...] = two_matmuls(acc, up, lambda o, g: nn(g, wb[l, o:o + FB, :])).astype(bf16)
            s_out_own(l, ch, b).start()
            g_out_own(l, ch, b).start()

            @pl.when((j == 3) & within(k, 4, 7))
            def _():
                start_all(w_reload(l))

            return carry

        each_layer(layer)

        @pl.when(k < 7)
        def _():
            tgt[j // PER, rows, :] = hc[...]
            h_out(j).start()

        @pl.when(k == 7)
        def _():
            @pl.when(j == 0)
            def _():
                rcopy(y_in, tgt.at[0], tsend.at[0], trecv.at[0], partner).wait_recv()

            @pl.when(j == 2)
            def _():
                lcopy(y_in, tgt.at[1], trecv.at[1]).wait()

            diff = hc[...].astype(f32) - tgt[j // PER, rows, :].astype(f32)
            es[j // PER, rows, :] = (diff * inv_total).astype(bf16)
            sq = jnp.sum((diff * diff).reshape(CH // 8, 8, D), axis=0)
            ltile[...] += sum(sq[:, i * 128:(i + 1) * 128] for i in range(D // 128))

            @pl.when(j == 3)
            def _():
                lmine[...] = ltile[...]

        h2_save(j).start()
        hT[0, ch // PER, :, rows] = nt(sel[...], hs[j // PER, rows, :]).astype(bf16)
        for l in range(1, NL):
            hT[l, ch // PER, :, rows] = nt(sel[...], sv[l - 1]).astype(bf16)
        h2_save(j).wait()
        for p in PEERS:
            h2_fwd(j, p).start()
        pre_h(t)

    def q_drain(t, li):
        @pl.when((li == flag(is_b_own(t))) & is_b_own(t - 1))
        def _():
            q_out_own(0, 0, flip(t)).wait()

    def f_oth(t):
        pr = f_pair(t)
        hi = t % PER

        @pl.when(is_f_own(t - 1))
        def _():
            f_drain_all()

        q_drain(t, 0)

        @pl.when((k < 7) & (t == 5 + 2 * flag(k == 6)))
        def _():
            for j in range(4):
                h_out(j).wait_send()

        h_in(pr, hi).wait()

        def layer(l, carry):
            b = (t + l) % PER
            wait_reload(t, l)

            if not isinstance(l, int):
                @pl.when((l == 1) & is_f_oth(t - 1))
                def _():
                    wait_all(f_outs(2, 0, b))

                @pl.when(l == 1)
                def _():
                    wait_pair(h2recv, pr)
                    h2_in(pr, hi).start()
                    pre_h(t)
                    pre_e(t)

                @pl.when(l == TOP)
                def _():
                    wait_all(f_outs(0, pr, b))
                    h2_in(pr, hi).wait()
                    hb[hi] = tgt[hi]

            h = hb[hi]
            hT[l, pr] = nt(sel[...], h).astype(bf16)

            def up(o):
                g, slope = gelu_and_slope(nt(h, wb[l, o:o + FB, :]))
                sb[b, :, o:o + FB] = slope
                g = g.astype(bf16)
                gb[b, :, o:o + FB] = g
                return g

            if isinstance(l, int):
                va[...] = h.astype(f32)
                hb[hi] = two_matmuls(va, up, lambda o, g: nt(g, wa[l, :, o:o + FB])).astype(bf16)
            else:
                for o in BLOCKS:
                    up(o)
            start_all(f_outs(l, pr, b))
            return carry

        each_layer(layer, peel=True)
        wait_all(f_outs(1, pr, flip(t)))

        @pl.when(is_loader(t + 1))
        def _():
            start_load(t + 1, 0, flip(t))

    def b_own(t):
        j = b_own_j(t)
        ch = own0 + j
        jp = j // PER
        first_load(t)
        wait_chunk(es, erecv, ch)
        for p in PEERS:
            e_fwd(j, p).start()
        ec[...] = es[jp, half(j), :]

        def layer(li, carry):
            l = TOP - li
            b = (t + li) % PER
            s_in_own(l, ch, b).wait()
            q_drain(t, li)

            @pl.when(li == TOP)
            def _():
                q_out_own(2, j, b).wait()
                q_out_own(1, j, 1 - b).wait()

            next_load(t, li, b)
            wait_reload(t, l)
            e = ec[...]

            sv[jnp.maximum(li - 1, 0)] = e
            acc = va.at[HEAD, :]
            acc[...] = e.astype(f32)

            def up(o):
                p = nn(e, wa[l, :, o:o + FB]).astype(bf16).astype(f32)
                qv = (p * sb[b, HEAD, o:o + FB]).astype(bf16)
                qb[b, HEAD, o:o + FB] = qv
                return qv

            ec[...] = two_matmuls(acc, up, lambda o, qv: nn(qv, wb[l, o:o + FB, :])).astype(bf16)
            q_out_own(l, j, b).start()
            return carry

        each_layer(layer)
        @pl.when(j >= 2)
        def _():
            e_out(j - 2).wait_send()

        eout[half(j), :] = ec[...]
        e_out(j).start()
        e1_save(j, 1).start()
        eTs[jp, 2, :, half(j)] = nt(sel[...], es[jp, half(j), :]).astype(bf16)
        for li in range(1, NL):
            eTs[jp, TOP - li, :, half(j)] = nt(sel[...], sv[li - 1]).astype(bf16)
        e1_save(j, 1).wait()

        @pl.when(j == jnp.where(k > 1, 1, 2))
        def _():
            for i in range(2):
                for p in PEERS:
                    e1_fwd(i, p).start()

        @pl.when(j == 3)
        def _():
            for i in range(2, 4):
                for p in PEERS:
                    e1_fwd(i, p).start()

        pre_e(t)
        pre_h(t)

    def wgrad(l, hTl, eTl, b):
        for o in range(0, F, FW):
            acc1[l, :, o:o + FW] += nn(hTl, qb[b, :, o:o + FW])
            acc2[l, :, o:o + FW] += nn(eTl, gb[b, :, o:o + FW])

    def bx_step(t):
        jp = bx_jp(t)
        pr = PER * q + jp
        eb[0] = es[jp]

        def layer(li, carry):
            l = TOP - li
            b = li % PER

            @pl.when(li == 1)
            def _():
                f_drain_all()
                start_all(b_ins(0, pr, 0))

            @pl.when(li == TOP)
            def _():
                wait_all(b_ins(0, pr, 0))
                for i in range(2):
                    sv[i] = eb[0, i * CH:(i + 1) * CH, :]

            e = eb[0]
            eT = nt(sel[...], e).astype(bf16)
            va[...] = e.astype(f32)

            def up(o):
                p = nt(e, wb[l, o:o + FB, :]).astype(bf16).astype(f32)
                qv = (p * sb[b, :, o:o + FB]).astype(bf16)
                qb[b, :, o:o + FB] = qv
                return qv

            eb[0] = two_matmuls(va, up, lambda o, qv: nt(qv, wa[l, :, o:o + FB])).astype(bf16)

            @pl.when(li == TOP)
            def _():
                @pl.when(jp == 1)
                def _():
                    for i in range(2):
                        e_out(i).wait_send()

                eout[...] = eb[0]
                for i in range(2):
                    e_out(PER * jp + i).start()
                for i in range(2):
                    e1_save(PER * jp + i, i).start()

            wgrad(l, hT[l, pr], eT, b)

            @pl.when(jp == 1)
            def _():
                start_all(w_reload(l))

            return carry

        each_layer(layer)
        for i in range(2):
            e1_save(PER * jp + i, i).wait()

        @pl.when(jp == 1)
        def _():
            for p in PEERS:
                l_peer(p).start()
            for pair in (0, 2):
                for fwd in (e_fwd, e1_fwd):
                    for i in (pair, pair + 1):
                        for p in PEERS:
                            fwd(i, p).start()
            pre_h(t)

    def w_step(t):
        jp = w_jp(t)
        q_drain(t, 0)

        @pl.when(is_f_oth(t - 1))
        def _():
            wait_all(f_outs(2, 0, flip(t)))

        start_load(t, 1, flip(t))

        def layer(li, carry):
            l = TOP - li
            b = (t + li) % PER
            wait_all(w_ins(l, jp, b))

            @pl.when(li == 1)
            def _():
                pre_h(t)
                pre_e(t)

            wgrad(l, hT[l, PER * q + jp], eTs[jp, l], b)

            @pl.when(li == 0)
            def _():
                start_load(t, 2, b)

            @pl.when(li == 1)
            def _():
                start_load(t + 1, 0, b)

            return carry

        each_layer(layer)

    half_own = pl.ds(pl.multiple_of(96 * c, 8), 96)
    half_oth = pl.ds(pl.multiple_of(96 * (1 - c), 8), 96)

    def final_copies(l):
        lg = NL * c + l
        return [
            rcopy(acc1.at[l, half_oth, :], out_up.at[lg], xo_s.at[l, 0], xo_r.at[l, 0], partner),
            rcopy(acc2.at[l, half_oth, :], out_down.at[lg], xo_s.at[l, 1], xo_r.at[l, 1], partner),
            lcopy(acc1.at[l, half_own, :], out_up.at[lg], lo_s.at[l, 0]),
            lcopy(acc2.at[l, half_own, :], out_down.at[lg], lo_s.at[l, 1]),
        ]

    def b_oth(t):
        pr = b_pair(t)
        ei = t % PER
        first_load(t)

        @pl.when(first & ((t == 11) | (t == 13)))
        def _():
            for i in range(2):
                j = t - 11 + i
                wait_chunk(es, erecv, own0 + j)
                for p in PEERS:
                    e_fwd(j, p).start()

        @pl.when(is_ob(t))
        def _():
            eb[ei] = es[ob_jp(t)]

        @pl.when(jnp.logical_not(is_ob(t)))
        def _():
            e_in(pr, ei).wait()

        def layer(li, carry):
            l = TOP - li
            b = (t + li) % PER
            wait_all(b_ins(l, pr, b))
            q_drain(t, li)
            next_load(t, li, b)

            if not isinstance(li, int):
                @pl.when(li == jnp.where(is_ob(t), 2, 1))
                def _():
                    pre_e(t)

                @pl.when((li == 1) & jnp.logical_not(first))
                def _():
                    wait_pair(e1recv, pr)
                    e1_in(pr, ei).start()

                @pl.when((li == TOP) & jnp.logical_not(first))
                def _():
                    e1_in(pr, ei).wait()
                    eb[ei] = tgt[ei]

            e = eb[ei]
            eT = nt(sel[...], e).astype(bf16)
            for o in range(0, F, FW):
                p = nn(e, wa[l, :, o:o + FW]).astype(bf16).astype(f32)
                qb[b, :, o:o + FW] = (p * sb[b, :, o:o + FW]).astype(bf16)
            if isinstance(li, int):
                for o in range(0, D, DW):
                    eb[ei, :, o:o + DW] = (e[:, o:o + DW].astype(f32) + nn(qb[b], wb[l, :, o:o + DW])).astype(bf16)
            wgrad(l, hT[l, pr], eT, b)

            if not isinstance(li, int):
                @pl.when((li == 1) & first)
                def _():
                    for o in range(0, D, DW):
                        eb[ei, :, o:o + DW] = (eb[ei, :, o:o + DW].astype(f32) + nn(qb[b], wb[l, :, o:o + DW])).astype(bf16)

            @pl.when(t == end)
            def _():
                start_all(final_copies(l))

            return carry

        each_layer(layer, peel=True)

        @pl.when(last & (t == 13))
        def _():
            for p in PEERS:
                qo = (q + 1 + p) % 4
                rcopy(lmine, lbuf.at[qo], lsend.at[p], lrecv.at[qo], peers[p]).wait_recv()
            lbuf[q] = lmine[...]
            tot = (lbuf[0] + lbuf[1]) + (lbuf[2] + lbuf[3])
            loss_out[...] = jnp.zeros((8, 128), f32) + jnp.sum(tot) * (0.5 * inv_total)
            for kk in range(7):
                l_out(kk).start()

    def step(t, carry):
        for test, run in ((is_tr, tr_step), (is_f_own, f_own), (is_f_oth, f_oth), (is_b_own, b_own), (is_bx, bx_step), (is_w, w_step), (is_b_oth, b_oth)):
            @pl.when(test(t))
            def _():
                run(t)

        return carry

    lax.fori_loop(0, NSTEP, step, 0)

    for j in range(4):
        for p in PEERS:
            h_fwd(j, p).wait_send()
            e_fwd(j, p).wait_send()
            h2_fwd(j, p).wait_send()

    @pl.when(k > 0)
    def _():
        for j in range(4):
            for p in PEERS:
                e1_fwd(j, p).wait_send()

    @pl.when(k > 0)
    def _():
        for j in range(2, 4):
            e_out(j).wait_send()

    @pl.when(k < 7)
    def _():
        l_out(0).wait_recv()

    @pl.when(k == 1)
    def _():
        xcopy(0).wait_send()
        xcopy(1).wait_send()

    @pl.when(k == 6)
    def _():
        tcopy().wait_send()

    @pl.when(k == 7)
    def _():
        for p in PEERS:
            l_peer(p).wait_send()
        for kk in range(7):
            l_out(kk).wait_send()

    for l in range(NL):
        lg = NL * (1 - c) + l
        rcopy(acc1.at[l, half_oth, :], out_up.at[lg], xo_s.at[l, 0], xo_r.at[l, 0], partner).wait_recv()
        rcopy(acc2.at[l, half_oth, :], out_down.at[lg], xo_s.at[l, 1], xo_r.at[l, 1], partner).wait_recv()
        r1, r2, l1, l2 = final_copies(l)
        r1.wait_send()
        r2.wait_send()
        l1.wait()
        l2.wait()


def solution(mesh):
    n_data = mesh.shape["data"]

    def per_device(inputs, targets, w_up, w_down):
        n_micro, n_tok, width = inputs.shape
        inv_total = 1.0 / (n_data * n_micro * n_tok)
        x = inputs.reshape(n_micro * n_tok, width)
        y = targets.reshape(n_micro * n_tok, width)
        V = pltpu.VMEM
        DMA = pltpu.SemaphoreType.DMA
        S = jax.ShapeDtypeStruct
        anyspec = pl.BlockSpec(memory_space=pl.ANY)
        pairs = 8
        half_grad = S((PER * NL, D // pairs, F), f32)
        rows = S((pairs, PR, D), bf16)
        two_rows = V((PER, PR, D), bf16)
        two_wide = V((PER, PR, F), bf16)
        grads = V((NL, DS, F), f32)
        tile = V((8, 128), f32)
        two, four, by_layer, chunks, fan = DMA((PER,)), DMA((4,)), DMA((NL, PER)), DMA((16,)), DMA((4, 3))
        outs = pl.pallas_call(
            functools.partial(kernel, inv_total),
            out_shape=(
                S((8, 128), f32), half_grad, half_grad,
                S((NL, pairs, PR, F), f32), S((NL, pairs, PR, F), bf16), S((NL, PER, PR, F), bf16),
                S((NL, D, F), bf16), S((NL, F, D), bf16), rows, rows, rows, rows,
            ),
            in_specs=[anyspec] * 4,
            out_specs=(pl.BlockSpec(memory_space=pltpu.VMEM),) + (anyspec,) * 11,
            scratch_shapes=[
                V((NL, D, F), bf16), V((NL, F, D), bf16), grads, grads, two_rows, two_rows,
                V((PER, PR, F), f32), two_wide, two_wide,
                V((NL, pairs, DS, PR), bf16), V((PER, NL, DS, PR), bf16),
                two_rows, two_rows, V((PR, D), bf16), two_rows, V((PER, CH, D), bf16), V((PR, D), f32),
                V((DS, D), bf16), tile, V((4, 8, 128), f32), tile,
                by_layer, by_layer, chunks, chunks, fan, fan, two, two, chunks, chunks, two, four, two,
                fan, fan, four, four, DMA((1,)), DMA((3,)), DMA((7,)), DMA,
            ] + [two] * 9 + [DMA((6,)), by_layer, by_layer, by_layer],
            compiler_params=pltpu.CompilerParams(collective_id=0, has_side_effects=True, vmem_limit_bytes=67043328),
            name="stack_step",
        )(x, y, w_up, w_down)
        return outs[0][0, 0], outs[1], jnp.swapaxes(outs[2], 1, 2)

    return jax.shard_map(
        per_device,
        mesh=mesh,
        in_specs=(P("data", None, None), P("data", None, None), P("stage", None, None), P("stage", None, None)),
        out_specs=(P(), P("stage", "data", None), P("stage", None, "data")),
        check_vma=False,
    )
```

time: 275 us -> 248 us (0.902)
  Pallas kernels: 261 us -> 236 us
    pallas_call x1, Pallas kernels: 261 us -> 236 us  [per_device(): pl.pallas_call(functools.partial(kernel, inv_total), out_shape=(S((8, 128...]
    unnamed x6 -> x4, local copies, waits for them, and re-layouts: 9.94 us -> 9.94 us
where the time goes in v3:
time: 248 us
  Pallas kernels  236 us (95%)
  local copies, waits for them, and re-layouts  11.1 us (4%)
    pallas_call x1, Pallas kernels, per_device(): pl.pallas_call(functools.partial(kernel, inv_total), out_shape=(S((8, 128...  236 us
    unnamed x4, local copies, waits for them, and re-layouts  9.94 us

profile of v3, /device:TPU:31, one launch (start us, length us, event | category | flops | bytes accessed | tf_op | source)
XLA Modules:
  0.0 247.8 jit_solution(11315042015556308750)
XLA Ops:
  0.6 236.1 %stack_step.1 = (f32[8,128]{1,0:T(8,128)}, f32[6,96,3072]{2,1,0:T(8,128)}, f32[6,96,3072]{2,1,0:T(8,128)}, f32[3,8,256,3072]{3,2,1,0:T(8,128)}, bf16[3,8,256,307...) custom-call(bf16[256,768]{1,0:T(8,128)(2,1)} %bitcast.5, ...), custom_call_target="tpu_custom_call" | custom-call | tf_op jit(solution)/shard_map/stack_step/pallas_call | solution.py:912
  236.7 1.2 slice.3
  237.9 0.0 copy-start
  237.9 7.0 %copy.9 = f32[6,96,3072]{2,1,0:T(8,128)} copy(f32[6,96,3072]{2,1,0:T(8,128)} %get-tuple-element.13) | data formatting | bytes 14155776
  244.9 0.0 copy-done
  244.9 3.0 %copy.10 = f32[6,3072,96]{1,2,0:T(8,128)} copy(f32[6,3072,96]{1,2,0:T(8,128)S(1)} %bitcast.4) | data formatting | bytes 14155776
Async XLA Ops:
  237.9 7.0 %copy-start = (f32[6,96,3072]{2,1,0:T(8,128)S(1)}, f32[6,96,3072]{2,1,0:T(8,128)}, u32[]{:S(2)}) copy-start(f32[6,96,3072]{2,1,0:T(8,128)} %get-tuple-element.8) | copy-start | bytes 21233668

commit v4 on v3

--- a/solution.py
+++ b/solution.py
@@ -45,10 +45,9 @@
 
 def gelu_and_slope(u):
     s = u * u
-    t = jnp.tanh(u * (C0 + C1 * s))
-    a = 1.0 + t
-    g = (0.5 * u) * a
-    return g, 0.5 * a + g * ((1.0 - t) * (C0 + (3.0 * C1) * s))
+    b = 0.5 + 0.5 * jnp.tanh(u * (C0 + C1 * s))
+    g = u * b
+    return g, b + (g * (1.0 - b)) * (2.0 * C0 + (6.0 * C1) * s)
 
 
 def two_matmuls(va, first, second):
@@ -242,6 +241,9 @@
         wait_chunk(hs, sems, PER * pr)
         wait_chunk(hs, sems, PER * pr + 1)
 
+    def ob_save(b):
+        return lcopy(eb.at[b], ex1.at[PER * q + 1], os_x.at[b])
+
     first, last = k == 0, k == 7
     mid = (k > 0) & (k < 7)
     high = k >= 4
@@ -437,7 +439,8 @@
 
             @pl.when((k == 6) & (j == 3) & (l == 1))
             def _():
-                start_load(t + 1, 0, flip(t))
+                for i in range(PER):
+                    start_load(t + 1, i, 1 - i)
 
             h = hc[...]
 
@@ -456,9 +459,14 @@
             s_out_own(l, ch, b).start()
             g_out_own(l, ch, b).start()
 
-            @pl.when((j == 3) & within(k, 4, 7))
+            @pl.when((j == 3) & within(k, 4, 6))
             def _():
                 start_all(w_reload(l))
+
+            @pl.when((j == 3) & (k == 6) & (l == TOP))
+            def _():
+                for i in reversed(range(NL)):
+                    start_all(w_reload(i))
 
             return carry
 
@@ -588,7 +596,11 @@
                 q_out_own(2, j, b).wait()
                 q_out_own(1, j, 1 - b).wait()
 
-            next_load(t, li, b)
+
+            @pl.when((li > 0) | jnp.logical_not(is_f_own(t - 1)))
+            def _():
+                next_load(t, li, b)
+
             wait_reload(t, l)
             e = ec[...]
 
@@ -756,12 +768,12 @@
     def b_oth(t):
         pr = b_pair(t)
         ei = t % PER
+        inner = jnp.logical_not(first) | (t > 16)
         first_load(t)
 
-        @pl.when(first & ((t == 11) | (t == 13)))
-        def _():
-            for i in range(2):
-                j = t - 11 + i
+        for j, at in ((0, 11), (1, 11), (2, 13), (3, 14)):
+            @pl.when(first & (t == at))
+            def _():
                 wait_chunk(es, erecv, own0 + j)
                 for p in PEERS:
                     e_fwd(j, p).start()
@@ -786,15 +798,19 @@
                 def _():
                     pre_e(t)
 
-                @pl.when((li == 1) & jnp.logical_not(first))
+                @pl.when((li == 1) & inner)
                 def _():
                     wait_pair(e1recv, pr)
                     e1_in(pr, ei).start()
 
-                @pl.when((li == TOP) & jnp.logical_not(first))
+                @pl.when((li == TOP) & inner)
                 def _():
                     e1_in(pr, ei).wait()
                     eb[ei] = tgt[ei]
+
+                @pl.when((li == TOP) & first & (t == 14))
+                def _():
+                    ob_save(ei).start()
 
             e = eb[ei]
             eT = nt(sel[...], e).astype(bf16)
@@ -807,7 +823,7 @@
             wgrad(l, hT[l, pr], eT, b)
 
             if not isinstance(li, int):
-                @pl.when((li == 1) & first)
+                @pl.when((li == 1) & jnp.logical_not(inner))
                 def _():
                     for o in range(0, D, DW):
                         eb[ei, :, o:o + DW] = (eb[ei, :, o:o + DW].astype(f32) + nn(qb[b], wb[l, :, o:o + DW])).astype(bf16)
@@ -819,6 +835,13 @@
             return carry
 
         each_layer(layer, peel=True)
+
+        @pl.when(first & (t == 14))
+        def _():
+            ob_save(ei).wait()
+            for j in range(2, 4):
+                for p in PEERS:
+                    e1_fwd(j, p).start()
 
         @pl.when(last & (t == 13))
         def _():
@@ -841,15 +864,19 @@
 
     lax.fori_loop(0, NSTEP, step, 0)
 
+    @pl.when(first)
+    def _():
+        wait_pair(e1recv, oth_pair(3))
+
     for j in range(4):
         for p in PEERS:
             h_fwd(j, p).wait_send()
             e_fwd(j, p).wait_send()
             h2_fwd(j, p).wait_send()
 
-    @pl.when(k > 0)
-    def _():
-        for j in range(4):
+    for j in range(4):
+        @pl.when((k > 0) | (j > 1))
+        def _():
             for p in PEERS:
                 e1_fwd(j, p).wait_send()
 

time: 248 us -> 245 us (0.988)
  Pallas kernels: 236 us -> 233 us
    pallas_call x1, Pallas kernels: 236 us -> 233 us  [per_device(): pl.pallas_call(functools.partial(kernel, inv_total), out_shape=(S((8, 128...]
where the time goes in v4:
time: 245 us
  Pallas kernels  233 us (95%)
  local copies, waits for them, and re-layouts  11.1 us (5%)
    pallas_call x1, Pallas kernels, per_device(): pl.pallas_call(functools.partial(kernel, inv_total), out_shape=(S((8, 128...  233 us
    unnamed x4, local copies, waits for them, and re-layouts  9.94 us

profile of v4, /device:TPU:31, one launch (start us, length us, event | category | flops | bytes accessed | tf_op | source)
XLA Modules:
  0.0 244.6 jit_solution(15082343727016513351)
XLA Ops:
  0.6 232.8 %stack_step.1 = (f32[8,128]{1,0:T(8,128)}, f32[6,96,3072]{2,1,0:T(8,128)}, f32[6,96,3072]{2,1,0:T(8,128)}, f32[3,8,256,3072]{3,2,1,0:T(8,128)}, bf16[3,8,256,307...) custom-call(bf16[256,768]{1,0:T(8,128)(2,1)} %bitcast.5, ...), custom_call_target="tpu_custom_call" | custom-call | tf_op jit(solution)/shard_map/stack_step/pallas_call | solution.py:939
  233.4 1.2 slice.3
  234.6 0.0 copy-start
  234.6 7.0 %copy.9 = f32[6,96,3072]{2,1,0:T(8,128)} copy(f32[6,96,3072]{2,1,0:T(8,128)} %get-tuple-element.13) | data formatting | bytes 14155776
  241.6 0.0 copy-done
  241.6 3.0 %copy.10 = f32[6,3072,96]{1,2,0:T(8,128)} copy(f32[6,3072,96]{1,2,0:T(8,128)S(1)} %bitcast.4) | data formatting | bytes 14155776
Async XLA Ops:
  234.6 7.0 %copy-start = (f32[6,96,3072]{2,1,0:T(8,128)S(1)}, f32[6,96,3072]{2,1,0:T(8,128)}, u32[]{:S(2)}) copy-start(f32[6,96,3072]{2,1,0:T(8,128)} %get-tuple-element.8) | copy-start | bytes 21233668

commit v5 on v4

--- a/solution.py
+++ b/solution.py
@@ -267,10 +267,13 @@
         return t // 6
 
     def is_f_own(t):
-        return within(t, 0, jnp.where(last, 6, 5)) & jnp.logical_not(is_tr(t) | is_bx(t))
+        return within(t, 0, jnp.where(last, 3, 5)) & jnp.logical_not(is_tr(t))
+
+    def is_f_two(t):
+        return last & (t == 4)
 
     def f_own_j(t):
-        return jnp.where(high, t - 1, t) - flag(last & (t > 3))
+        return jnp.where(high, t - 1, t)
 
     def is_b_own(t):
         return mid & (within(t, 5 + m, 7 + m) | within(t, 8 + m, 10 + m))
@@ -417,6 +420,57 @@
         reload(NL - 1)
         pre_h(t)
 
+    def top_grads(jp, rows, h):
+        diff = h.astype(f32) - tgt[jp, rows, :].astype(f32)
+        es[jp, rows, :] = (diff * inv_total).astype(bf16)
+        sq = jnp.sum((diff * diff).reshape(h.shape[0] // 8, 8, D), axis=0)
+        ltile[...] += sum(sq[:, i:i + 128] for i in range(0, D, 128))
+
+    def f_two(t):
+        pr = PER * q + 1
+        for j in range(2, 4):
+            wait_chunk(hs, hrecv, own0 + j)
+            for p in PEERS:
+                h_fwd(j, p).start()
+        hb[0] = hs[1]
+
+        def layer(l, carry):
+            b = l % PER
+
+            @pl.when(l == TOP)
+            def _():
+                wait_all(f_outs(0, pr, 0))
+                for i in range(PER):
+                    sv[i] = hb[0, i * CH:(i + 1) * CH, :]
+
+            h = hb[0]
+            hT[l, pr] = nt(sel[...], h).astype(bf16)
+            va[...] = h.astype(f32)
+
+            def up(o):
+                g, slope = gelu_and_slope(nn(h, wa[l, :, o:o + FB]))
+                sb[b, :, o:o + FB] = slope
+                g = g.astype(bf16)
+                gb[b, :, o:o + FB] = g
+                return g
+
+            hb[0] = two_matmuls(va, up, lambda o, g: nn(g, wb[l, o:o + FB, :])).astype(bf16)
+            start_all(f_outs(l, pr, b))
+            return carry
+
+        each_layer(layer)
+        lcopy(y_in, tgt.at[1], trecv.at[1]).wait()
+        for i in range(PER):
+            rows = slice(i * CH, (i + 1) * CH)
+            top_grads(1, rows, hb[0, rows, :])
+        lmine[...] = ltile[...]
+        saves = [lcopy(sv.at[i], hx2.at[pr, pl.ds(i * CH, CH), :], os_x.at[i]) for i in range(PER)]
+        start_all(saves)
+        wait_all(saves)
+        for j in range(2, 4):
+            for p in PEERS:
+                h2_fwd(j, p).start()
+
     def f_own(t):
         j = f_own_j(t)
         ch = own0 + j
@@ -483,18 +537,7 @@
             def _():
                 rcopy(y_in, tgt.at[0], tsend.at[0], trecv.at[0], partner).wait_recv()
 
-            @pl.when(j == 2)
-            def _():
-                lcopy(y_in, tgt.at[1], trecv.at[1]).wait()
-
-            diff = hc[...].astype(f32) - tgt[j // PER, rows, :].astype(f32)
-            es[j // PER, rows, :] = (diff * inv_total).astype(bf16)
-            sq = jnp.sum((diff * diff).reshape(CH // 8, 8, D), axis=0)
-            ltile[...] += sum(sq[:, i * 128:(i + 1) * 128] for i in range(D // 128))
-
-            @pl.when(j == 3)
-            def _():
-                lmine[...] = ltile[...]
+            top_grads(j // PER, rows, hc[...])
 
         h2_save(j).start()
         hT[0, ch // PER, :, rows] = nt(sel[...], hs[j // PER, rows, :]).astype(bf16)
@@ -662,7 +705,15 @@
 
             @pl.when(li == 1)
             def _():
-                f_drain_all()
+                @pl.when(jp == 0)
+                def _():
+                    f_drain_all()
+
+                @pl.when(jp == 1)
+                def _():
+                    for bb in range(PER):
+                        wait_all(f_outs(0, pr, bb))
+
                 start_all(b_ins(0, pr, 0))
 
             @pl.when(li == TOP)
@@ -855,7 +906,7 @@
                 l_out(kk).start()
 
     def step(t, carry):
-        for test, run in ((is_tr, tr_step), (is_f_own, f_own), (is_f_oth, f_oth), (is_b_own, b_own), (is_bx, bx_step), (is_w, w_step), (is_b_oth, b_oth)):
+        for test, run in ((is_tr, tr_step), (is_f_own, f_own), (is_f_oth, f_oth), (is_b_own, b_own), (is_bx, bx_step), (is_f_two, f_two), (is_w, w_step), (is_b_oth, b_oth)):
             @pl.when(test(t))
             def _():
                 run(t)

time: 245 us -> 244 us (level)
  no operation moved by 1% of the time
where the time goes in v5:
time: 244 us
  Pallas kernels  232 us (95%)
  local copies, waits for them, and re-layouts  11.1 us (5%)
    pallas_call x1, Pallas kernels, per_device(): pl.pallas_call(functools.partial(kernel, inv_total), out_shape=(S((8, 128...  232 us
    unnamed x4, local copies, waits for them, and re-layouts  9.94 us

profile of v5, /device:TPU:31, one launch (start us, length us, event | category | flops | bytes accessed | tf_op | source)
XLA Modules:
  0.0 243.5 jit_solution(2181086452912061052)
XLA Ops:
  0.6 231.8 %stack_step.1 = (f32[8,128]{1,0:T(8,128)}, f32[6,96,3072]{2,1,0:T(8,128)}, f32[6,96,3072]{2,1,0:T(8,128)}, f32[3,8,256,3072]{3,2,1,0:T(8,128)}, bf16[3,8,256,307...) custom-call(bf16[256,768]{1,0:T(8,128)(2,1)} %bitcast.5, ...), custom_call_target="tpu_custom_call" | custom-call | tf_op jit(solution)/shard_map/stack_step/pallas_call | solution.py:990
  232.4 1.2 slice.3
  233.6 0.0 copy-start
  233.6 7.0 %copy.9 = f32[6,96,3072]{2,1,0:T(8,128)} copy(f32[6,96,3072]{2,1,0:T(8,128)} %get-tuple-element.13) | data formatting | bytes 14155776
  240.6 0.0 copy-done
  240.6 3.0 %copy.10 = f32[6,3072,96]{1,2,0:T(8,128)} copy(f32[6,3072,96]{1,2,0:T(8,128)S(1)} %bitcast.4) | data formatting | bytes 14155776
Async XLA Ops:
  233.6 7.0 %copy-start = (f32[6,96,3072]{2,1,0:T(8,128)S(1)}, f32[6,96,3072]{2,1,0:T(8,128)}, u32[]{:S(2)}) copy-start(f32[6,96,3072]{2,1,0:T(8,128)} %get-tuple-element.8) | copy-start | bytes 21233668
